TPU v7x, 32 devices: a whole 2x2x4 slice. The times are simulated.
32 devices in a mesh: dp: 2 (over x), tp: 4 (over z), ep: 4 (over y, core).
Axes of the slice: x: 2, y: 2, z: 4, core: 2. Of those that a mesh axis runs over, the one named last changes fastest.
Arguments:
- hidden: bfloat16 [512, 1536], P(('dp', 'ep')), parts along dimension 0
- seq_lens: int32 [512], P(('dp', 'ep')), parts along dimension 0
- rope_cos: float32 [512, 32], P(('dp', 'ep')), parts along dimension 0
- rope_sin: float32 [512, 32], P(('dp', 'ep')), parts along dimension 0
- ln1_scale: bfloat16 [1536], replicated
- ln1_bias: bfloat16 [1536], replicated
- w_qkv: bfloat16 [1536, 2560], P(None, 'tp')
- b_qkv: bfloat16 [2560], P('tp')
- w_out: bfloat16 [1536, 1536], P('tp')
- b_out: bfloat16 [1536], replicated
- k_cache: bfloat16 [512, 512, 8, 64], P(('dp', 'ep'), None, 'tp'), parts along dimension 0
- v_cache: bfloat16 [512, 512, 8, 64], P(('dp', 'ep'), None, 'tp'), parts along dimension 0
- ln2_scale: bfloat16 [1536], replicated
- ln2_bias: bfloat16 [1536], replicated
- w_router: bfloat16 [1536, 40], replicated
- expert_ids: int32 [512, 8], P(('dp', 'ep')), parts along dimension 0
- w_gate: bfloat16 [40, 1536, 512], P('ep', None, 'tp')
- w_up: bfloat16 [40, 1536, 512], P('ep', None, 'tp')
- w_down: bfloat16 [40, 512, 1536], P('ep', 'tp')
Outputs:
- output 1: bfloat16 [512, 1536], P(('dp', 'ep')), parts along dimension 0
- output 2: bfloat16 [512, 512, 8, 64], P(('dp', 'ep'), None, 'tp'), parts along dimension 0
- output 3: bfloat16 [512, 512, 8, 64], P(('dp', 'ep'), None, 'tp'), parts along dimension 0
There are 2 independent parts. A program takes and returns all parts, laid end to end along the dimension named above; an argument that names none is the same for every part.
All inputs are finite; a program needn't handle non-finite values.
Results may differ from a plain program's by a relative error of at most 0.01133.
Values are sent between devices in bfloat16 or wider.
A program may use at most 1 GiB of HBM per device.

v0:
```python
import jax
import jax.numpy as jnp
from jax import lax
from jax.sharding import PartitionSpec as P

EPS = 1e-5


def layer_norm(values, ln_scale, ln_bias):
    vals_f32 = values.astype(jnp.float32)
    row_mean = jnp.mean(vals_f32, axis=-1, keepdims=True)
    centered = vals_f32 - row_mean
    row_var = jnp.mean(centered * centered, axis=-1, keepdims=True)
    normed = centered * lax.rsqrt(row_var + EPS)
    return (normed * ln_scale.astype(jnp.float32) + ln_bias.astype(jnp.float32)).astype(jnp.bfloat16)


def apply_rope(values, cos_part, sin_part):
    half_dim = values.shape[-1] // 2
    vals_f32 = values.astype(jnp.float32)
    first_half = vals_f32[..., :half_dim]
    second_half = vals_f32[..., half_dim:]
    rotated = jnp.concatenate([first_half * cos_part - second_half * sin_part, second_half * cos_part + first_half * sin_part], axis=-1)
    return rotated.astype(jnp.bfloat16)


def attention_part(normed, seq_lens, rope_cos, rope_sin, w_qkv, b_qkv, w_out, k_cache, v_cache):
    n_batch, s_max, n_groups, head_dim = k_cache.shape
    q_per = w_qkv.shape[1] // (n_groups * head_dim) - 2
    qkv_rows = (jnp.dot(normed, w_qkv, preferred_element_type=jnp.float32) + b_qkv.astype(jnp.float32)).astype(jnp.bfloat16)
    qkv_rows = qkv_rows.reshape(n_batch, n_groups, q_per + 2, head_dim)
    queries = apply_rope(qkv_rows[:, :, :q_per], rope_cos[:, None, None, :], rope_sin[:, None, None, :])
    key_new = apply_rope(qkv_rows[:, :, q_per], rope_cos[:, None, :], rope_sin[:, None, :])
    value_new = qkv_rows[:, :, q_per + 1]
    positions = jnp.arange(s_max)
    write_mask = (positions[None, :] == seq_lens[:, None])[:, :, None, None]
    k_cache_out = jnp.where(write_mask, key_new[:, None], k_cache)
    v_cache_out = jnp.where(write_mask, value_new[:, None], v_cache)
    scores = jnp.einsum('bgqh,bsgh->bgqs', queries, k_cache_out, preferred_element_type=jnp.float32) * head_dim ** -0.5
    in_range = positions[None, None, None, :] <= seq_lens[:, None, None, None]
    attn_probs = jax.nn.softmax(jnp.where(in_range, scores, -jnp.inf), axis=-1).astype(jnp.bfloat16)
    context = jnp.einsum('bgqs,bsgh->bgqh', attn_probs, v_cache_out, preferred_element_type=jnp.float32).astype(jnp.bfloat16)
    attn_part = jnp.dot(context.reshape(n_batch, n_groups * q_per * head_dim), w_out, preferred_element_type=jnp.float32)
    return attn_part, k_cache_out, v_cache_out


def route_tables(expert_ids, gate_probs, first_expert, n_exp, capacity):
    id_match = expert_ids[..., None] == (first_expert + jnp.arange(n_exp))
    chosen_mask = jnp.sum(id_match.astype(jnp.int32), axis=-2)
    slot_rank = jnp.cumsum(chosen_mask, axis=-2) - chosen_mask
    slot_of = jnp.swapaxes(jnp.where(chosen_mask > 0, slot_rank, -1), -1, -2)
    dispatch = (slot_of[..., None, :] == jnp.arange(capacity)[:, None]).astype(jnp.bfloat16)
    gate_dense = jnp.sum(jnp.where(id_match, gate_probs[..., None].astype(jnp.float32), 0.0), axis=-2)
    combine = dispatch * jnp.swapaxes(gate_dense, -1, -2)[..., None, :].astype(jnp.bfloat16)
    return dispatch, combine


def expert_ffn(routed_rows, w_gate, w_up, w_down):
    gate_pre = jnp.einsum('secd,edf->escf', routed_rows, w_gate, preferred_element_type=jnp.float32)
    up_pre = jnp.einsum('secd,edf->escf', routed_rows, w_up, preferred_element_type=jnp.float32)
    hidden_act = (jax.nn.silu(gate_pre) * up_pre).astype(jnp.bfloat16)
    return jnp.einsum('escf,efd->escd', hidden_act, w_down, preferred_element_type=jnp.float32)


def solution(mesh):
    n_ep = mesh.shape['ep']
    token_rows = P(('dp', 'ep'), None)
    token_vec = P(('dp', 'ep'))
    cache_spec = P(('dp', 'ep'), None, 'tp', None)
    expert_in = P('ep', None, 'tp')
    expert_down = P('ep', 'tp', None)

    def device_step(hidden, seq_lens, rope_cos, rope_sin, ln1_scale, ln1_bias, w_qkv, b_qkv, w_out, b_out, k_cache, v_cache, ln2_scale, ln2_bias, w_router, expert_ids, w_gate, w_up, w_down):
        n_batch, d_model = hidden.shape
        e_local = w_gate.shape[0]
        n_exp = e_local * n_ep
        top_k = expert_ids.shape[1]
        capacity = (2 * top_k * n_batch + n_exp - 1) // n_exp
        normed = layer_norm(hidden, ln1_scale, ln1_bias)
        attn_part, k_cache_out, v_cache_out = attention_part(normed, seq_lens, rope_cos, rope_sin, w_qkv, b_qkv, w_out, k_cache, v_cache)
        attn_sum = lax.psum(attn_part.astype(jnp.bfloat16), 'tp')
        hidden_mid = (hidden.astype(jnp.float32) + attn_sum.astype(jnp.float32) + b_out.astype(jnp.float32)).astype(jnp.bfloat16)
        normed2 = layer_norm(hidden_mid, ln2_scale, ln2_bias)
        logits = jnp.dot(normed2, w_router, preferred_element_type=jnp.float32)
        gate_probs = jax.nn.softmax(jnp.take_along_axis(logits, expert_ids, axis=1), axis=-1).astype(jnp.bfloat16)
        dispatch, combine = route_tables(expert_ids, gate_probs, 0, n_exp, capacity)
        outgoing = jnp.einsum('ecb,bd->ecd', dispatch, normed2, preferred_element_type=jnp.float32).astype(jnp.bfloat16)
        received = lax.all_to_all(outgoing, 'ep', 0, 0, tiled=True).reshape(n_ep, e_local, capacity, d_model)
        down_part = expert_ffn(received, w_gate, w_up, w_down).astype(jnp.bfloat16)
        expert_out = lax.psum(down_part, 'tp')
        returned = lax.all_to_all(expert_out, 'ep', 1, 0, tiled=True).reshape(n_exp, capacity, d_model)
        moe_sum = jnp.einsum('ecb,ecd->bd', combine, returned, preferred_element_type=jnp.float32)
        hidden_out = (hidden_mid.astype(jnp.float32) + moe_sum).astype(jnp.bfloat16)
        return hidden_out, k_cache_out, v_cache_out

    in_specs = (token_rows, token_vec, token_rows, token_rows, P(), P(), P(None, 'tp'), P('tp'), P('tp', None), P(), cache_spec, cache_spec, P(), P(), P(), token_rows, expert_in, expert_in, expert_down)
    return jax.shard_map(device_step, mesh=mesh, in_specs=in_specs, out_specs=(token_rows, cache_spec, cache_spec), check_vma=False)
```

profile of v0, /device:TPU:0, one launch (start us, length us, event | category | flops | bytes accessed | tf_op | source)
XLA Modules:
  0.0 353.3 jit_solution(16761540212200430800)
XLA Ops:
  7.2 0.0 copy-start
  7.2 0.0 all-reduce.3.cloned.1.call-start
  7.2 1.2 convert_reduce_fusion.1
  8.4 1.2 fusion.52
  9.6 0.7 convert_element_type.103
  10.3 0.7 convert_element_type.100
  11.0 0.7 convert_element_type.101
  11.7 0.0 copy-done
  11.7 1.4 fusion.36
  13.1 0.2 copy.89
  13.3 0.8 copy.91
  14.1 0.8 copy.92
  14.9 0.8 iota_compare_fusion.4
  15.7 0.8 subtract_convert_fusion.1
  16.4 0.1 copy.93
  16.6 0.1 copy.95
  16.7 0.1 copy.112
  16.8 0.2 subtract_convert_fusion
  17.1 12.0 %broadcast_select_fusion.1 = (bf16[64,512,2,64]{1,3,2,0:T(8,128)(2,1)}, bf16[64,512,2,64]{1,3,2,0:T(8,128)(2,1)}) fusion(bf16[64,512,2,64]{1,3,2,0:T(8,128)(2,1)} %param.29, pred[64,512]{1,0:T(8,128)(4,1)S(1)} %get-tuple-element.14, bf16[64,2,64]{2,1,0:T(2,128)(2,1)S(1)} %copy.93, bf16[64,512,2,64]{1,3,2,0:T(8,128)(2,1)} %param.30, ...), kind=kLoop, calls=%fused_computation.3 | loop fusion | flops 8388608 | bytes 33619968 | tf_op jit(solution)/shard_map/jit(_where)/select_n | solution.py:37
  29.1 5.0 %fusion.84 = (f32[64,2,3]{2,1,0:T(2,128)S(1)}, f32[64,2,3,512]{3,2,1,0:T(4,128)S(1)}) fusion(bf16[64,512,2,64]{1,3,2,0:T(8,128)(2,1)} %get-tuple-element.11, pred[64,512]{1,0:T(8,128)(4,1)S(1)} %get-tuple-element.13, bf16[64,2,3,32]{3,2,1,0:T(4,128)(2,1)S(1)} %get-tuple-element.6, bf16[64,2,3,32]{3,2,1,0:T(4,128)(2,1)S(1)} %get-tuple-element.5), kind=kOutput, calls=%fused_computation.100 | convolution fusion | flops 26051072 | bytes 9258496 | tf_op jit(solution)/shard_map/sub | solution.py:41
  34.1 0.0 copy-start.4
  34.1 0.0 copy-start.6
  34.2 0.0 copy-start.7
  34.2 0.0 copy-start.8
  34.2 0.0 copy-start.5
  34.2 0.0 copy-start.3
  34.2 5.8 %convolution_convert_fusion.3 = bf16[64,2,3,64]{3,2,1,0:T(4,128)(2,1)S(1)} fusion(bf16[64,512,2,64]{1,3,2,0:T(8,128)(2,1)} %get-tuple-element.12, f32[64,2,3,512]{3,2,1,0:T(4,128)S(1)} %get-tuple-element.16, f32[64,2,3]{2,1,0:T(2,128)S(1)} %get-tuple-element.15), kind=kOutput, calls=%fused_computation.25 | convolution fusion | flops 25583616 | bytes 9225728 | tf_op jit(solution)/shard_map/bgqs,bsgh->bgqh/dot_general | solution.py:42
  40.0 0.2 reshape.152
  40.2 0.0 copy-done.4
  40.2 1.0 convolution_convert_fusion.2
  41.2 0.0 all-reduce.3.cloned.1.call-update
  41.2 0.0 all-reduce.5.cloned.1.call-start
  41.3 0.0 copy-done.6
  41.3 0.0 copy-done.7
  41.3 0.0 copy-done.8
  41.3 0.0 copy-done.5
  41.4 0.1 copy.96
  41.5 0.1 reduce_window_sum.11
  41.6 0.1 copy.99
  41.6 37.3 %all-reduce.3.cloned.1.call-done = bf16[64,1536]{1,0:T(8,128)(2,1)} async-done(((bf16[64,1536]{1,0:T(8,128)(2,1)}), bf16[64,1536]{1,0:T(8,128)(2,1)}) %all-reduce.3.cloned.1.call-update) | async-done | bytes 196624 | tf_op jit(solution)/shard_map/psum | solution.py:81
  78.9 0.0 copy-done.3
  78.9 1.1 convert_reduce_fusion
  80.0 0.2 fusion.48
  80.3 1.1 convolution_convert_fusion.1
  81.4 1.1 copy.102
  82.5 0.0 copy-start.9
  82.5 48.1 %all_to_all.20 = bf16[40,26,1536]{2,1,0:T(8,128)(2,1)S(1)} all-to-all(bf16[40,26,1536]{2,1,0:T(8,128)(2,1)S(1)} %copy.102), channel_id=1, replica_groups=mesh['dp'=2,'tp'=4,'ep'=4] {'ep'}, dimensions={0} | all-to-all | bytes 6389760 | tf_op jit(solution)/shard_map/all_to_all | solution.py:88
  130.6 1.9 copy-done.2
  132.5 0.0 copy-done.9
  132.5 1.3 fusion.4
  133.8 8.5 %convolution_convert_fusion = bf16[10,4,26,1536]{3,2,1,0:T(8,128)(2,1)} fusion(bf16[10,128,1536]{2,1,0:T(8,128)(2,1)} %param.37, bf16[10,1536,128]{2,1,0:T(8,128)(2,1)} %param.36, bf16[4,10,26,1536]{3,2,1,0:T(8,128)(2,1)} %bitcast.60, f32[10,4,26,128]{3,2,1,0:T(8,128)S(1)} %fusion.4), kind=kOutput, calls=%fused_computation.4 | convolution fusion | flops 820285440 | bytes 14786560 | tf_op jit(solution)/shard_map/escf,efd->escd/dot_general | solution.py:62
  142.3 0.0 all-reduce.5.cloned.1.call-update
  142.3 144.4 %all-reduce.5.cloned.1.call-done = bf16[10,4,26,1536]{3,2,1,0:T(8,128)(2,1)} async-done(((bf16[10,4,26,1536]{3,2,1,0:T(8,128)(2,1)}), bf16[10,4,26,1536]{3,2,1,0:T(8,128)(2,1)}) %all-reduce.5.cloned.1.call-update) | async-done | bytes 3194896 | tf_op jit(solution)/shard_map/psum | solution.py:90
  286.7 4.5 %copy.105 = bf16[10,4,26,1536]{3,2,0,1:T(8,128)(2,1)} copy(bf16[10,4,26,1536]{3,2,1,0:T(8,128)(2,1)} %all-reduce.5.cloned.1.call-done) | data formatting | bytes 6389760 | tf_op jit(solution)/shard_map/psum | solution.py:90
  291.2 5.1 %all-to-all-start.1 = ((bf16[10,4,26,1536]{3,2,0,1:T(8,128)(2,1)}), bf16[10,4,26,1536]{3,2,0,1:T(8,128)(2,1)}, u32[]{:S(2)}, u32[]{:S(2)}) async-start(bf16[10,4,26,1536]{3,2,0,1:T(8,128)(2,1)} %copy.105), calls=%async_computation.1 | async-start | bytes 7864320 | tf_op jit(solution)/shard_map/all_to_all | solution.py:91
  296.3 0.1 copy.100
  296.4 0.1 reshape.157
  296.5 0.3 fusion.81
  296.8 0.0 copy-start.1
  296.8 3.9 %gather_fusion = f32[512]{0:T(512)S(1)} fusion(f32[64,40]{0,1:T(8,128)S(1)} %fusion.81, s32[512]{0:T(512)S(1)} %reshape.157), kind=kCustom, calls=%fused_computation | custom fusion | bytes 8192 | tf_op jit(solution)/shard_map/jit(take_along_axis)/gather | solution.py:85
  300.7 0.1 reshape.160
  300.8 0.1 copy.101
  300.9 40.4 %all-to-all-done.1 = bf16[10,4,26,1536]{3,2,0,1:T(8,128)(2,1)} async-done(((bf16[10,4,26,1536]{3,2,0,1:T(8,128)(2,1)}), bf16[10,4,26,1536]{3,2,0,1:T(8,128)(2,1)}, u32[]{:S(2)}, u32[]{:S(2)}) %all-to-all-start.1) | async-done | bytes 3194912 | tf_op jit(solution)/shard_map/all_to_all | solution.py:91
  341.4 5.1 %fusion.16 = bf16[64,1536]{1,0:T(8,128)(2,1)} fusion(bf16[40,26,1536]{2,1,0:T(8,128)(2,1)} %bitcast.17, bf16[64,1536]{1,0:T(8,128)(2,1)S(1)} %get-tuple-element.4, s32[40,64]{1,0:T(8,128)S(1)} %copy.99, bf16[40,64]{1,0:T(8,128)(2,1)S(1)} %bitcast.63), kind=kOutput, calls=%fused_computation.17 | convolution fusion | flops 204900352 | bytes 3603456 | tf_op jit(solution)/shard_map/ecb,ecd->bd/dot_general | solution.py:92
  (22 shorter events, 0.2 us)
Async XLA Ops:
  7.2 4.5 %copy-start = (bf16[1536,640]{1,0:T(8,128)(2,1)S(1)}, bf16[1536,640]{1,0:T(8,128)(2,1)}, u32[]{:S(2)}) copy-start(bf16[1536,640]{1,0:T(8,128)(2,1)} %param.25) | copy-start | bytes 5898244
  7.2 71.7 %all-reduce.3.cloned.1.call-start = ((), (), s32[]{:S(2)}) async-start(), calls=%async_computation.2 | async-start | bytes 393216 | tf_op jit(solution)/shard_map/psum | solution.py:81
  34.1 6.0 %copy-start.4 = (bf16[384,1536]{1,0:T(8,128)(2,1)S(1)}, bf16[384,1536]{1,0:T(8,128)(2,1)}, u32[]{:S(2)}) copy-start(bf16[384,1536]{1,0:T(8,128)(2,1)} %param.27) | copy-start | bytes 3538948
  34.1 7.1 %copy-start.6 = (bf16[1536]{0:T(1024)(128)(2,1)S(1)}, bf16[1536]{0:T(1024)(128)(2,1)}, u32[]{:S(2)}) copy-start(bf16[1536]{0:T(1024)(128)(2,1)} %param.31) | copy-start | bytes 9220
  34.2 7.1 %copy-start.7 = (bf16[1536]{0:T(1024)(128)(2,1)S(1)}, bf16[1536]{0:T(1024)(128)(2,1)}, u32[]{:S(2)}) copy-start(bf16[1536]{0:T(1024)(128)(2,1)} %param.32) | copy-start | bytes 9220
  34.2 7.2 %copy-start.8 = (bf16[1536]{0:T(1024)(128)(2,1)S(1)}, bf16[1536]{0:T(1024)(128)(2,1)}, u32[]{:S(2)}) copy-start(bf16[1536]{0:T(1024)(128)(2,1)} %param.28) | copy-start | bytes 9220
  34.2 7.2 %copy-start.5 = (s32[64,8]{0,1:T(8,128)S(1)}, s32[64,8]{0,1:T(8,128)}, u32[]{:S(2)}) copy-start(s32[64,8]{0,1:T(8,128)} %param.34) | copy-start | bytes 6148
  34.2 44.7 %copy-start.3 = (bf16[64,1536]{1,0:T(8,128)(2,1)S(1)}, bf16[64,1536]{1,0:T(8,128)(2,1)}, u32[]{:S(2)}) copy-start(bf16[64,1536]{1,0:T(8,128)(2,1)} %param.19) | copy-start | bytes 589828
  41.2 245.5 %all-reduce.5.cloned.1.call-start = ((), (), s32[]{:S(2)}) async-start(), calls=%async_computation.3 | async-start | bytes 7864320 | tf_op jit(solution)/shard_map/psum | solution.py:90
  82.5 50.0 %copy-start.9 = (bf16[10,1536,128]{2,1,0:T(8,128)(2,1)S(1)}, bf16[10,1536,128]{2,1,0:T(8,128)(2,1)}, u32[]{:S(2)}) copy-start(bf16[10,1536,128]{2,1,0:T(8,128)(2,1)} %param.35) | copy-start | bytes 11796484
  130.6 1.9 copy-start.2
  291.2 5.3 %copy-start.10 = (bf16[1536,40]{0,1:T(8,128)(2,1)S(1)}, bf16[1536,40]{0,1:T(8,128)(2,1)}, u32[]{:S(2)}) copy-start(bf16[1536,40]{0,1:T(8,128)(2,1)} %param.33) | copy-start | bytes 368644
  291.2 50.2 %all-to-all-start.1 = ((bf16[10,4,26,1536]{3,2,0,1:T(8,128)(2,1)}), bf16[10,4,26,1536]{3,2,0,1:T(8,128)(2,1)}, u32[]{:S(2)}, u32[]{:S(2)}) async-start(bf16[10,4,26,1536]{3,2,0,1:T(8,128)(2,1)} %copy.105), calls=%async_computation.1 | async-start | bytes 7864320 | tf_op jit(solution)/shard_map/all_to_all | solution.py:91
  296.8 49.7 %copy-start.1 = (bf16[1536,640]{1,0:T(8,128)(2,1)S(1)}, bf16[1536,640]{1,0:T(8,128)(2,1)}, u32[]{:S(2)}) copy-start(bf16[1536,640]{1,0:T(8,128)(2,1)} %param.25) | copy-start | bytes 5898244
Sparse Core Ops, SparseCore 0:
  41.3 37.5 all-reduce.2
  142.5 144.2 all-reduce.4
where the time goes:
time: 354 us; the launch traced here: 353 us
  waiting for transfers between devices  222 us (63%)
  blocking collectives  48.1 us (14%)
  matrix products  29.5 us (8%)
  other arithmetic  19.8 us (6%)
  between operations  14.4 us (4%)
  local copies, waits for them, and re-layouts  14.2 us (4%)
  starting transfers between devices  5.19 us (1%)
    psum x1, waiting for transfers between devices, device_step(): expert_out = lax.psum(down_part, 'tp')  144 us
    all_to_all x1, blocking collectives, device_step(): lax.all_to_all(outgoing, 'ep', 0, 0, tiled=True)  48.1 us
    all_to_all x1, waiting for transfers between devices, device_step(): lax.all_to_all(expert_out, 'ep', 1, 0, tiled=True)  40.4 us
    psum x1, waiting for transfers between devices, device_step(): attn_sum = lax.psum(attn_part.astype(jnp.bfloat16), 'tp')  37.3 us
    select_n x1, other arithmetic, attention_part(): k_cache_out = jnp.where(write_mask, key_new[:, None], k_cache)  12 us
    dot_general x1, matrix products, expert_ffn(): jnp.einsum('escf,efd->escd', hidden_act, w_down, preferred_element_type=j...  8.54 us
  transfers between devices with their start and end apart: 3, of which 3 were waited for; matrix products, arithmetic and copies ran while one was open for 1% of the time, Pallas kernels for 0%

commit v1 on v0

v1 whole, which is shorter than its diff:
```python
import functools

import jax
import jax.numpy as jnp
from jax import lax
from jax.experimental import pallas as pl
from jax.experimental.pallas import tpu as pltpu
from jax.sharding import PartitionSpec as P

EPS = 1e-5
F32 = jnp.float32
BF16 = jnp.bfloat16
MESH = pl.DeviceIdType.MESH
VMEM_LIMIT = 60 * 1024 * 1024
NT = (((1,), (1,)), ((), ()))
BB = 8
COLS = 3


def normalize(vals_f32, ln_scale, ln_bias):
    row_mean = jnp.mean(vals_f32, axis=-1, keepdims=True)
    centered = vals_f32 - row_mean
    row_var = jnp.mean(centered * centered, axis=-1, keepdims=True)
    normed = centered * lax.rsqrt(row_var + EPS)
    return (normed * ln_scale + ln_bias).astype(BF16)


def row_of(vec_ref):
    return vec_ref[...].astype(F32)[None, :]


def attention_kernel(lens_ref, hid_ref, cos_ref, sin_ref, scale_ref, bias_ref, bqkv_ref, wqkv_hbm, k_hbm, v_hbm,
                     ctx_ref, ko_hbm, vo_hbm, k_buf, v_buf, w_buf, q_buf, kn_buf, vn_buf, c_buf, w_sem, k_sem, v_sem, ko_sem, vo_sem):
    n_rows = hid_ref.shape[0]
    n_blocks = n_rows // BB
    s_max = k_buf.shape[2]
    w_copy = pltpu.make_async_copy(wqkv_hbm, w_buf, w_sem)
    w_copy.start()

    def fetch(i):
        rows = pl.ds(i * BB, BB)
        return (pltpu.make_async_copy(k_hbm.at[rows], k_buf.at[rows], k_sem.at[i]),
                pltpu.make_async_copy(v_hbm.at[rows], v_buf.at[rows], v_sem.at[i]))

    def flush(i):
        rows = pl.ds(i * BB, BB)
        return (pltpu.make_async_copy(k_buf.at[rows], ko_hbm.at[rows], ko_sem.at[i]),
                pltpu.make_async_copy(v_buf.at[rows], vo_hbm.at[rows], vo_sem.at[i]))

    for i in range(n_blocks):
        for copy in fetch(i):
            copy.start()

    normed = normalize(hid_ref[...].astype(F32), row_of(scale_ref), row_of(bias_ref))
    w_copy.wait()
    qkv = jnp.dot(normed, w_buf[...], preferred_element_type=F32) + row_of(bqkv_ref)
    qkv = qkv.astype(BF16).astype(F32)
    qkv = jnp.concatenate([qkv, jnp.zeros((128 - n_rows, qkv.shape[1]), F32)], axis=0)
    feats = qkv.T
    cos_t = jnp.concatenate([cos_ref[...], jnp.zeros((32, 128 - n_rows), F32)], axis=1)
    sin_t = jnp.concatenate([sin_ref[...], jnp.zeros((32, 128 - n_rows), F32)], axis=1)

    def rotate(base):
        u, w = feats[base:base + 32], feats[base + 32:base + 64]
        return jnp.concatenate([u * cos_t - w * sin_t, w * cos_t + u * sin_t], axis=0).astype(BF16).astype(F32)

    zeros = jnp.zeros((64, 128), F32)
    for g in range(2):
        for j in range(3):
            q_rot = rotate(g * 320 + j * 64)
            both = jnp.concatenate([q_rot, zeros] if g == 0 else [zeros, q_rot], axis=0)
            q_buf[pl.ds(g * 3 + j, n_rows, stride=8), :] = both.T[:n_rows]
    for r in (6, 7):
        q_buf[pl.ds(r, n_rows, stride=8), :] = jnp.zeros((n_rows, 128), F32)
    k_new = jnp.concatenate([rotate(192), rotate(320 + 192)], axis=0)
    v_new = jnp.concatenate([feats[256:320], feats[320 + 256:320 + 320]], axis=0)
    for i in range(n_blocks):
        kn_buf[i] = k_new if i == 0 else pltpu.roll(k_new, 128 - i * BB, 1)
        vn_buf[i] = v_new if i == 0 else pltpu.roll(v_new, 128 - i * BB, 1)

    def block(i, carry):
        for copy in fetch(i):
            copy.wait()
        k_cols, v_cols = kn_buf[i], vn_buf[i]
        lane = lax.broadcasted_iota(jnp.int32, (128, 128), 1)
        position = lax.broadcasted_iota(jnp.int32, (8, s_max), 1)
        scores = []
        for j in range(BB):
            b = i * BB + j
            pos = lens_ref[b]
            first = pl.multiple_of((pos // 128) * 128, 128)
            hit = lane == pos - first
            window = pl.ds(first, 128)
            k_buf[b, :, window] = jnp.where(hit, k_cols[:, j:j + 1], k_buf[b, :, window].astype(F32)).astype(BF16)
            v_buf[b, :, window] = jnp.where(hit, v_cols[:, j:j + 1], v_buf[b, :, window].astype(F32)).astype(BF16)
            rows = pl.ds(pl.multiple_of(b * 8, 8), 8)
            one = jnp.dot(q_buf[rows, :].astype(BF16), k_buf[b], preferred_element_type=F32) * 0.125
            scores.append(jnp.where(position <= pos, one, -jnp.inf))
        scores = jnp.concatenate(scores, axis=0)
        top = jnp.max(scores, axis=1, keepdims=True)
        weights = jnp.exp(scores - top)
        probs = weights * (1.0 / jnp.sum(weights, axis=1, keepdims=True))
        for j in range(BB):
            b = i * BB + j
            rows = pl.ds(pl.multiple_of(b * 8, 8), 8)
            c_buf[rows, :] = lax.dot_general(probs[j * 8:j * 8 + 8].astype(BF16), v_buf[b], NT, preferred_element_type=F32)
        for copy in flush(i):
            copy.start()
        return carry

    lax.fori_loop(0, n_blocks, block, 0)
    heads = [c_buf[pl.ds(r, n_rows, stride=8), :] for r in range(6)]
    low = lax.broadcasted_iota(jnp.int32, (n_rows, 128), 1) < 64
    ctx_ref[:, 0:128] = jnp.where(low, heads[0], pltpu.roll(heads[1], 64, 1)).astype(BF16)
    ctx_ref[:, 128:256] = jnp.where(low, heads[2], heads[3]).astype(BF16)
    ctx_ref[:, 256:384] = jnp.where(low, pltpu.roll(heads[4], 64, 1), heads[5]).astype(BF16)
    for i in range(n_blocks):
        for copy in flush(i):
            copy.wait()


def moe_kernel(hid_ref, ctx_ref, bout_ref, scale_ref, bias_ref, wr_ref, ids_ref, wout_hbm, wg_hbm, wu_hbm, wd_hbm, out_ref,
               wout, wgu, wd, wr, part_f, part_b, rs_recv, x1_buf, h2, ids_buf, act, lo, hi, d_recv, y_send, y_recv, t_f, t_b, z_recv, o_buf,
               wsem, ssem, rsem):
    z, ep = lax.axis_index("tp"), lax.axis_index("ep")
    n_rows, d_model = hid_ref.shape
    n_exp = wgu.shape[0]
    width = d_model // COLS
    z_peers = [lax.rem(z + dz, 4) for dz in (1, 2, 3)]
    y_peer = lax.rem(ep + 2, 4)
    partner = ep + 1 - 2 * lax.rem(ep, 2)
    diagonal = 3 - ep
    barrier = pltpu.get_barrier_semaphore()
    for peer in z_peers:
        pl.semaphore_signal(barrier, inc=1, device_id={"tp": peer}, device_id_type=MESH)
    for peer in (y_peer, partner, diagonal):
        pl.semaphore_signal(barrier, inc=1, device_id={"ep": peer}, device_id_type=MESH)

    loads = [pltpu.make_async_copy(wout_hbm, wout, wsem.at[0])]
    for e in range(n_exp):
        loads.append(pltpu.make_async_copy(wg_hbm.at[e], wgu.at[e, :, 0:128], wsem.at[1 + 2 * e]))
        loads.append(pltpu.make_async_copy(wu_hbm.at[e], wgu.at[e, :, 128:256], wsem.at[2 + 2 * e]))
    loads.append(pltpu.make_async_copy(wd_hbm, wd, wsem.at[1 + 2 * n_exp]))
    for load in loads:
        load.start()

    sent = []

    def send(src, dst, slot, device):
        copy = pltpu.make_async_remote_copy(src_ref=src, dst_ref=dst, send_sem=ssem.at[slot], recv_sem=rsem.at[slot],
                                            device_id=device, device_id_type=MESH)
        copy.start()
        sent.append(copy)
        return copy

    loads[0].wait()
    part = jnp.dot(ctx_ref[...], wout[...], preferred_element_type=F32)
    part_f[...] = part
    part_b[...] = part.astype(BF16)
    wr[...] = jnp.concatenate([wr_ref[...], jnp.zeros((128 - wr_ref.shape[0], d_model), BF16)], axis=0)
    ids_buf[0] = ids_ref[...]
    pl.semaphore_wait(barrier, 6)

    def rows_of(index):
        return pl.ds(pl.multiple_of(index * 16, 16), 16)

    mine = rows_of(z)
    slot = 0
    rs = []
    for dz in range(3):
        rs.append(send(part_b.at[rows_of(z_peers[dz])], rs_recv.at[dz], slot, {"tp": z_peers[dz]}))
        slot += 1
    id_copies = []
    for shard, peer in ((1, y_peer), (2, partner), (3, diagonal)):
        id_copies.append(send(ids_ref, ids_buf.at[shard], slot, {"ep": peer}))
        slot += 1
    for copy in rs:
        copy.wait_recv()
    total = part_f[mine, :] + rs_recv[0].astype(F32) + rs_recv[1].astype(F32) + rs_recv[2].astype(F32)
    x1 = (hid_ref[mine, :].astype(F32) + total + row_of(bout_ref)).astype(BF16).astype(F32)
    x1_buf[...] = x1
    h2[mine, :] = normalize(x1, row_of(scale_ref), row_of(bias_ref))

    def piece(shard, index):
        return h2.at[pl.ds(pl.multiple_of(shard * n_rows + index * 16, 16), 16)]

    from_z, from_y, from_p = [], [], []
    for dz in range(3):
        from_z.append(send(piece(0, z), piece(0, z), slot, {"tp": z_peers[dz]}))
        slot += 1

    def pass_on(index):
        nonlocal slot
        from_y.append(send(piece(0, index), piece(1, index), slot, {"ep": y_peer}))
        slot += 1
        from_p.append(send(piece(0, index), piece(2, index), slot, {"ep": partner}))
        slot += 1

    z_order = [z] + [lax.rem(z + 4 - dz, 4) for dz in (1, 2, 3)]
    pass_on(z)
    for dz in range(3):
        from_z[dz].wait_recv()
        pass_on(z_order[dz + 1])

    def masks(shard):
        picks = ids_buf[shard]
        expert = lax.broadcasted_iota(jnp.int32, (128, n_rows), 0)
        hit = jnp.zeros((128, n_rows), F32)
        for k in range(picks.shape[0]):
            hit = jnp.where(expert == picks[k:k + 1, :], 1.0, hit)
        return hit.T

    def up(shard):
        rows = h2[shard * n_rows:(shard + 1) * n_rows, :]
        logits = lax.dot_general(rows, wr[...], NT, preferred_element_type=F32)
        picked = masks(shard) > 0.5
        logits = jnp.where(picked, logits, -jnp.inf)
        shifted = jnp.exp(logits - jnp.max(logits, axis=1, keepdims=True))
        gates = (shifted / jnp.sum(shifted, axis=1, keepdims=True)).astype(BF16).astype(F32)
        gates = pltpu.roll(gates, lax.rem(128 - ep * n_exp, 128), 1)
        for e in range(n_exp):
            if shard == 0:
                loads[1 + 2 * e].wait()
                loads[2 + 2 * e].wait()
            pre = jnp.dot(rows, wgu[e], preferred_element_type=F32)
            gate_pre, up_pre = pre[:, :128], pre[:, 128:]
            hidden = (gate_pre * jax.nn.sigmoid(gate_pre) * up_pre).astype(BF16).astype(F32)
            act[shard * n_rows:(shard + 1) * n_rows, e * 128:(e + 1) * 128] = (hidden * gates[:, e:e + 1]).astype(BF16)

    up(0)
    from_pp = []
    for k in range(4):
        from_y[k].wait_recv()
        index = z_order[k]
        from_pp.append(send(piece(1, index), piece(3, index), slot, {"ep": partner}))
        slot += 1
    for k in range(4):
        from_p[k].wait_recv()
    for copy in id_copies:
        copy.wait_recv()
    up(2)
    up(1)
    for k in range(4):
        from_pp[k].wait_recv()
    up(3)
    loads[-1].wait()

    def cols(n):
        return pl.ds(n * width, width)

    from_d, from_yy, from_zz, from_o = [], [], [], []

    def reduce_pair(n):
        nonlocal slot
        from_d[n].wait_recv()
        y_send[:, cols(n)] = (lo[64:128, cols(n)] + d_recv[64:128, cols(n)].astype(F32)).astype(BF16)
        from_yy.append(send(y_send.at[:, cols(n)], y_recv.at[:, cols(n)], slot, {"ep": y_peer}))
        slot += 1

    for n in range(COLS):
        hi[:, cols(n)] = jnp.dot(act[128:256, :], wd[:, cols(n)], preferred_element_type=F32).astype(BF16)
        from_d.append(send(hi.at[:, cols(n)], d_recv.at[:, cols(n)], slot, {"ep": partner}))
        slot += 1
        if n > 0:
            reduce_pair(n - 1)
        lo[:, cols(n)] = jnp.dot(act[0:128, :], wd[:, cols(n)], preferred_element_type=F32)
    reduce_pair(COLS - 1)
    for n in range(COLS):
        from_yy[n].wait_recv()
        t = lo[0:64, cols(n)] + d_recv[0:64, cols(n)].astype(F32) + y_recv[:, cols(n)].astype(F32)
        t_f[:, cols(n)] = t
        t_b[:, cols(n)] = t.astype(BF16)
        group = []
        for dz in range(3):
            group.append(send(t_b.at[rows_of(z_peers[dz]), cols(n)], z_recv.at[dz, :, cols(n)], slot, {"tp": z_peers[dz]}))
            slot += 1
        from_zz.append(group)
    for n in range(COLS):
        for copy in from_zz[n]:
            copy.wait_recv()
        moe = t_f[mine, cols(n)] + z_recv[0, :, cols(n)].astype(F32) + z_recv[1, :, cols(n)].astype(F32) + z_recv[2, :, cols(n)].astype(F32)
        o_buf[mine, cols(n)] = (x1_buf[:, cols(n)] + moe).astype(BF16)
        for dz in range(3):
            from_o.append(send(o_buf.at[mine, cols(n)], o_buf.at[mine, cols(n)], slot, {"tp": z_peers[dz]}))
            slot += 1
    for copy in from_o:
        copy.wait_recv()
    out_ref[...] = o_buf[...]
    for copy in sent:
        copy.wait_send()


N_SLOTS = 3 + 3 + 3 + 8 + 4 + COLS * 2 + COLS * 6


def solution(mesh):
    token_rows = P(('dp', 'ep'), None)
    token_vec = P(('dp', 'ep'))
    cache_spec = P(('dp', 'ep'), None, 'tp', None)
    expert_in = P('ep', None, 'tp')
    expert_down = P('ep', 'tp', None)
    vm = pl.BlockSpec(memory_space=pltpu.VMEM)
    sm = pl.BlockSpec(memory_space=pltpu.SMEM)
    anyspace = pl.BlockSpec(memory_space=pl.ANY)

    def device_step(hidden, seq_lens, rope_cos, rope_sin, ln1_scale, ln1_bias, w_qkv, b_qkv, w_out, b_out, k_cache, v_cache, ln2_scale, ln2_bias, w_router, expert_ids, w_gate, w_up, w_down):
        n, d = hidden.shape
        _, s_max, groups, head = k_cache.shape
        feat = groups * head
        n_exp = w_gate.shape[0]
        k_in = k_cache.transpose(0, 2, 3, 1).reshape(n, feat, s_max)
        v_in = v_cache.transpose(0, 2, 3, 1).reshape(n, feat, s_max)
        ctx, k_out, v_out = pl.pallas_call(
            attention_kernel,
            out_shape=(jax.ShapeDtypeStruct((n, 384), BF16), jax.ShapeDtypeStruct(k_in.shape, BF16), jax.ShapeDtypeStruct(v_in.shape, BF16)),
            in_specs=[sm, vm, vm, vm, vm, vm, vm, anyspace, anyspace, anyspace],
            out_specs=(vm, anyspace, anyspace),
            scratch_shapes=[
                pltpu.VMEM(k_in.shape, BF16), pltpu.VMEM(v_in.shape, BF16), pltpu.VMEM(w_qkv.shape, BF16),
                pltpu.VMEM((n * 8, 128), F32), pltpu.VMEM((n // BB, 128, 128), F32), pltpu.VMEM((n // BB, 128, 128), F32), pltpu.VMEM((n * 8, 128), F32),
                pltpu.SemaphoreType.DMA, pltpu.SemaphoreType.DMA((n // BB,)), pltpu.SemaphoreType.DMA((n // BB,)),
                pltpu.SemaphoreType.DMA((n // BB,)), pltpu.SemaphoreType.DMA((n // BB,)),
            ],
            compiler_params=pltpu.CompilerParams(vmem_limit_bytes=VMEM_LIMIT),
            name="attention",
        )(seq_lens, hidden, rope_cos.T, rope_sin.T, ln1_scale, ln1_bias, b_qkv, w_qkv, k_in, v_in)
        rows = lambda r, t: pltpu.VMEM((r, d), t)
        hidden_out = pl.pallas_call(
            moe_kernel,
            out_shape=jax.ShapeDtypeStruct((n, d), BF16),
            in_specs=[vm] * 7 + [anyspace] * 4,
            out_specs=vm,
            scratch_shapes=[
                pltpu.VMEM(w_out.shape, BF16), pltpu.VMEM((n_exp, d, 256), BF16), pltpu.VMEM((n_exp * 128, d), BF16), rows(128, BF16),
                rows(64, F32), rows(64, BF16), pltpu.VMEM((3, 16, d), BF16), rows(16, F32), rows(256, BF16), pltpu.VMEM((4, 8, n), jnp.int32),
                pltpu.VMEM((256, n_exp * 128), BF16), rows(128, F32), rows(128, BF16), rows(128, BF16), rows(64, BF16), rows(64, BF16),
                rows(64, F32), rows(64, BF16), pltpu.VMEM((3, 16, d), BF16), rows(64, BF16),
                pltpu.SemaphoreType.DMA((2 * n_exp + 2,)), pltpu.SemaphoreType.DMA((N_SLOTS,)), pltpu.SemaphoreType.DMA((N_SLOTS,)),
            ],
            compiler_params=pltpu.CompilerParams(vmem_limit_bytes=VMEM_LIMIT, collective_id=0, has_side_effects=True),
            name="moe",
        )(hidden, ctx, b_out, ln2_scale, ln2_bias, w_router.T, expert_ids.T, w_out, w_gate, w_up, w_down.reshape(n_exp * 128, d))
        unfold = lambda c: c.reshape(n, groups, head, s_max).transpose(0, 3, 1, 2)
        return hidden_out, unfold(k_out), unfold(v_out)

    in_specs = (token_rows, token_vec, token_rows, token_rows, P(), P(), P(None, 'tp'), P('tp'), P('tp', None), P(), cache_spec, cache_spec, P(), P(), P(), token_rows, expert_in, expert_in, expert_down)
    return jax.shard_map(device_step, mesh=mesh, in_specs=in_specs, out_specs=(token_rows, cache_spec, cache_spec), check_vma=False)
```

time: 354 us -> 63.1 us (0.18)
  waiting for transfers between devices: 222 us -> 0 us
  Pallas kernels: 0 us -> 60.6 us
  blocking collectives: 48.1 us -> 0 us
  matrix products: 29.5 us -> 0 us
  other arithmetic: 19.8 us -> 0 us
  between operations: 14.4 us -> 0.65 us
  local copies, waits for them, and re-layouts: 14.2 us -> 1.62 us
  starting transfers between devices: 5.19 us -> 0 us
    psum x2 -> x0, waiting for transfers between devices: 182 us -> none  [the longest x1 144 us: device_step(): expert_out = lax.psum(down_part, 'tp')]
    pallas_call x0 -> x2, Pallas kernels: none -> 60.6 us  [the longest x1 44.3 us: device_step(): pl.pallas_call(moe_kernel, out_shape=jax.ShapeDtypeStruct((n, d), BF16),...]
    all_to_all x1 -> x0, blocking collectives: 48.1 us -> none  [device_step(): lax.all_to_all(outgoing, 'ep', 0, 0, tiled=True)]
    all_to_all x1 -> x0, waiting for transfers between devices: 40.4 us -> none  [device_step(): lax.all_to_all(expert_out, 'ep', 1, 0, tiled=True)]
    dot_general x8 -> x0, matrix products: 24.5 us -> none  [the longest x1 8.54 us: expert_ffn(): jnp.einsum('escf,efd->escd', hidden_act, w_down, preferred_element_type=j...]
    select_n x2 -> x0, other arithmetic: 12 us -> none  [the longest x1 12 us: attention_part(): k_cache_out = jnp.where(write_mask, key_new[:, None], k_cache)]
    all_to_all x1 -> x0, starting transfers between devices: 5.11 us -> none  [device_step(): lax.all_to_all(expert_out, 'ep', 1, 0, tiled=True)]
    sub x1 -> x0, matrix products: 5.03 us -> none  [attention_part(): jax.nn.softmax(jnp.where(in_range, scores, -jnp.inf), axis=-1)]
  transfers between devices with their start and end apart: 3 -> 0, of which waited for: 3 -> 0; matrix products, arithmetic and copies ran while one was open for 1% -> 0% of each run, Pallas kernels for 0% -> 0%
where the time goes in v1:
time: 63.1 us; the launch traced here: 62.9 us
  Pallas kernels  60.6 us (96%)
  local copies, waits for them, and re-layouts  1.62 us (3%)
  between operations  0.65 us (1%)
    pallas_call x1, Pallas kernels, device_step(): pl.pallas_call(moe_kernel, out_shape=jax.ShapeDtypeStruct((n, d), BF16),...  44.3 us
    pallas_call x1, Pallas kernels, device_step(): pl.pallas_call(attention_kernel, out_shape=(jax.ShapeDtypeStruct((n, 384)...  16.3 us
    unnamed x1, local copies, waits for them, and re-layouts  1.62 us

profile of v1, /device:TPU:0, one launch (start us, length us, event | category | flops | bytes accessed | tf_op | source)
XLA Modules:
  0.0 62.9 jit_solution(15459996909075570742)
XLA Ops:
  0.6 16.3 %attention.1 = (bf16[64,384]{1,0:T(8,128)(2,1)}, bf16[64,128,512]{2,1,0:T(8,128)(2,1)}, bf16[64,128,512]{2,1,0:T(8,128)(2,1)}) custom-call(s32[64]{0:T(128)} %lens_ref.1, bf16[64,1536]{1,0:T(8,128)(2,1)} %hid_ref.3, f32[32,64]{1,0:T(8,128)} %bitcast.21, f32[32,64]{1,0:T(8,128)} %bitcast.22, bf16[1536]{0:T(1024)(128)(2,1)} %scale_ref.2, ...), custom_call_target="tpu_custom_call" | custom-call | tf_op jit(solution)/shard_map/attention/pallas_call | solution.py:313
  17.0 44.3 %moe.1 = bf16[64,1536]{1,0:T(8,128)(2,1)} custom-call(bf16[64,1536]{1,0:T(8,128)(2,1)} %hid_ref.3, bf16[64,384]{1,0:T(8,128)(2,1)} %get-tuple-element.6.ctx_ref, bf16[1536]{0:T(1024)(128)(2,1)} %bout_ref.1, bf16[1536]{0:T(1024)(128)(2,1)} %scale_ref.3, bf16[1536]{0:T(1024)(128)(2,1)} %bias_ref.3, bf16[40,1536]{1,0:T(8,128)(2,1)} %bitcast.20, ...), custom_call_target="tpu_custom_call" | custom-call | tf_op jit(solution)/shard_map/moe/pallas_call | solution.py:328
  61.3 1.6 %copy.23 = bf16[64,1536]{1,0:T(8,128)(2,1)} copy(bf16[64,1536]{1,0:T(8,128)(2,1)} %moe.1) | data formatting | bytes 393216

commit v2 on v1

--- a/solution.py
+++ b/solution.py
@@ -11,7 +11,8 @@
 F32 = jnp.float32
 BF16 = jnp.bfloat16
 MESH = pl.DeviceIdType.MESH
-VMEM_LIMIT = 60 * 1024 * 1024
+VMEM_LIMIT = 66_600_000
+MOE_LIMIT = 66_200_000
 NT = (((1,), (1,)), ((), ()))
 BB = 8
 COLS = 3
@@ -29,13 +30,18 @@
     return vec_ref[...].astype(F32)[None, :]
 
 
-def attention_kernel(lens_ref, hid_ref, cos_ref, sin_ref, scale_ref, bias_ref, bqkv_ref, wqkv_hbm, k_hbm, v_hbm,
-                     ctx_ref, ko_hbm, vo_hbm, k_buf, v_buf, w_buf, q_buf, kn_buf, vn_buf, c_buf, w_sem, k_sem, v_sem, ko_sem, vo_sem):
+def attention_kernel(lens_hbm, hid_hbm, cos_hbm, sin_hbm, scale_hbm, bias_hbm, bqkv_hbm, wqkv_hbm, k_hbm, v_hbm,
+                     ctx_ref, ko_hbm, vo_hbm, lens_ref, hid_ref, cos_ref, sin_ref, scale_ref, bias_ref, bqkv_ref,
+                     k_buf, v_buf, w_buf, q_buf, kn_buf, vn_buf, c_buf, in_sem, w_sem, k_sem, v_sem, ko_sem, vo_sem):
     n_rows = hid_ref.shape[0]
     n_blocks = n_rows // BB
     s_max = k_buf.shape[2]
+    smalls = ((hid_hbm, hid_ref), (scale_hbm, scale_ref), (bias_hbm, bias_ref), (bqkv_hbm, bqkv_ref), (cos_hbm, cos_ref), (sin_hbm, sin_ref),
+              (lens_hbm, lens_ref))
+    small_copies = [pltpu.make_async_copy(src, dst, in_sem.at[i]) for i, (src, dst) in enumerate(smalls)]
     w_copy = pltpu.make_async_copy(wqkv_hbm, w_buf, w_sem)
-    w_copy.start()
+    for copy in small_copies[:3] + [w_copy] + small_copies[3:]:
+        copy.start()
 
     def fetch(i):
         rows = pl.ds(i * BB, BB)
@@ -51,6 +57,8 @@
         for copy in fetch(i):
             copy.start()
 
+    for copy in small_copies:
+        copy.wait()
     normed = normalize(hid_ref[...].astype(F32), row_of(scale_ref), row_of(bias_ref))
     w_copy.wait()
     qkv = jnp.dot(normed, w_buf[...], preferred_element_type=F32) + row_of(bqkv_ref)
@@ -104,11 +112,12 @@
             b = i * BB + j
             rows = pl.ds(pl.multiple_of(b * 8, 8), 8)
             c_buf[rows, :] = lax.dot_general(probs[j * 8:j * 8 + 8].astype(BF16), v_buf[b], NT, preferred_element_type=F32)
+        return carry
+
+    lax.fori_loop(0, n_blocks, block, 0)
+    for i in range(n_blocks):
         for copy in flush(i):
             copy.start()
-        return carry
-
-    lax.fori_loop(0, n_blocks, block, 0)
     heads = [c_buf[pl.ds(r, n_rows, stride=8), :] for r in range(6)]
     low = lax.broadcasted_iota(jnp.int32, (n_rows, 128), 1) < 64
     ctx_ref[:, 0:128] = jnp.where(low, heads[0], pltpu.roll(heads[1], 64, 1)).astype(BF16)
@@ -300,7 +309,6 @@
     expert_in = P('ep', None, 'tp')
     expert_down = P('ep', 'tp', None)
     vm = pl.BlockSpec(memory_space=pltpu.VMEM)
-    sm = pl.BlockSpec(memory_space=pltpu.SMEM)
     anyspace = pl.BlockSpec(memory_space=pl.ANY)
 
     def device_step(hidden, seq_lens, rope_cos, rope_sin, ln1_scale, ln1_bias, w_qkv, b_qkv, w_out, b_out, k_cache, v_cache, ln2_scale, ln2_bias, w_router, expert_ids, w_gate, w_up, w_down):
@@ -312,13 +320,15 @@
         v_in = v_cache.transpose(0, 2, 3, 1).reshape(n, feat, s_max)
         ctx, k_out, v_out = pl.pallas_call(
             attention_kernel,
-            out_shape=(jax.ShapeDtypeStruct((n, 384), BF16), jax.ShapeDtypeStruct(k_in.shape, BF16), jax.ShapeDtypeStruct(v_in.shape, BF16)),
-            in_specs=[sm, vm, vm, vm, vm, vm, vm, anyspace, anyspace, anyspace],
+            out_shape=(pltpu.VMEM((n, 384), BF16), jax.ShapeDtypeStruct(k_in.shape, BF16), jax.ShapeDtypeStruct(v_in.shape, BF16)),
+            in_specs=[anyspace] * 10,
             out_specs=(vm, anyspace, anyspace),
             scratch_shapes=[
+                pltpu.SMEM((n,), jnp.int32), pltpu.VMEM((n, d), BF16), pltpu.VMEM((32, n), F32), pltpu.VMEM((32, n), F32),
+                pltpu.VMEM((d,), BF16), pltpu.VMEM((d,), BF16), pltpu.VMEM(b_qkv.shape, BF16),
                 pltpu.VMEM(k_in.shape, BF16), pltpu.VMEM(v_in.shape, BF16), pltpu.VMEM(w_qkv.shape, BF16),
                 pltpu.VMEM((n * 8, 128), F32), pltpu.VMEM((n // BB, 128, 128), F32), pltpu.VMEM((n // BB, 128, 128), F32), pltpu.VMEM((n * 8, 128), F32),
-                pltpu.SemaphoreType.DMA, pltpu.SemaphoreType.DMA((n // BB,)), pltpu.SemaphoreType.DMA((n // BB,)),
+                pltpu.SemaphoreType.DMA((7,)), pltpu.SemaphoreType.DMA, pltpu.SemaphoreType.DMA((n // BB,)), pltpu.SemaphoreType.DMA((n // BB,)),
                 pltpu.SemaphoreType.DMA((n // BB,)), pltpu.SemaphoreType.DMA((n // BB,)),
             ],
             compiler_params=pltpu.CompilerParams(vmem_limit_bytes=VMEM_LIMIT),
@@ -327,7 +337,7 @@
         rows = lambda r, t: pltpu.VMEM((r, d), t)
         hidden_out = pl.pallas_call(
             moe_kernel,
-            out_shape=jax.ShapeDtypeStruct((n, d), BF16),
+            out_shape=pltpu.VMEM((n, d), BF16),
             in_specs=[vm] * 7 + [anyspace] * 4,
             out_specs=vm,
             scratch_shapes=[
@@ -337,7 +347,7 @@
                 rows(64, F32), rows(64, BF16), pltpu.VMEM((3, 16, d), BF16), rows(64, BF16),
                 pltpu.SemaphoreType.DMA((2 * n_exp + 2,)), pltpu.SemaphoreType.DMA((N_SLOTS,)), pltpu.SemaphoreType.DMA((N_SLOTS,)),
             ],
-            compiler_params=pltpu.CompilerParams(vmem_limit_bytes=VMEM_LIMIT, collective_id=0, has_side_effects=True),
+            compiler_params=pltpu.CompilerParams(vmem_limit_bytes=MOE_LIMIT, collective_id=0, has_side_effects=True),
             name="moe",
         )(hidden, ctx, b_out, ln2_scale, ln2_bias, w_router.T, expert_ids.T, w_out, w_gate, w_up, w_down.reshape(n_exp * 128, d))
         unfold = lambda c: c.reshape(n, groups, head, s_max).transpose(0, 3, 1, 2)

time: 63.1 us -> 64.9 us (1.029)
  Pallas kernels: 60.6 us -> 62.8 us
    pallas_call x2, Pallas kernels: 60.6 us -> 62.8 us  [the longest x1 43.6 us: device_step(): pl.pallas_call(moe_kernel, out_shape=pltpu.VMEM((n, d), BF16), in_specs=[...]
    unnamed x1 -> x3, local copies, waits for them, and re-layouts: 1.62 us -> 1.29 us
where the time goes in v2:
time: 64.9 us; the launch traced here: 64.8 us
  Pallas kernels  62.8 us (97%)
  local copies, waits for them, and re-layouts  1.29 us (2%)
  between operations  0.66 us (1%)
    pallas_call x1, Pallas kernels, device_step(): pl.pallas_call(moe_kernel, out_shape=pltpu.VMEM((n, d), BF16), in_specs=[...  43.6 us
    pallas_call x1, Pallas kernels, device_step(): pl.pallas_call(attention_kernel, out_shape=(pltpu.VMEM((n, 384), BF16), j...  19.2 us

profile of v2, /device:TPU:0, one launch (start us, length us, event | category | flops | bytes accessed | tf_op | source)
XLA Modules:
  0.0 64.8 jit_solution(2197999105577082889)
XLA Ops:
  0.6 19.2 %attention.1 = (bf16[64,384]{1,0:T(8,128)(2,1)S(1)}, bf16[64,128,512]{2,1,0:T(8,128)(2,1)}, bf16[64,128,512]{2,1,0:T(8,128)(2,1)}) custom-call(s32[64]{0:T(128)} %lens_hbm.1, bf16[64,1536]{1,0:T(8,128)(2,1)} %hid_ref.1, f32[32,64]{1,0:T(8,128)} %bitcast.21, f32[32,64]{1,0:T(8,128)} %bitcast.22, bf16[1536]{0:T(1024)(128)(2,1)} %scale_hbm.1, ...), custom_call_target="tpu_custom_call" | custom-call | tf_op jit(solution)/shard_map/attention/pallas_call | solution.py:321
  19.9 0.0 copy-start
  19.9 0.6 copy-done
  20.5 43.6 %moe.1 = bf16[64,1536]{1,0:T(8,128)(2,1)S(1)} custom-call(bf16[64,1536]{1,0:T(8,128)(2,1)} %hid_ref.1, bf16[64,384]{1,0:T(8,128)(2,1)} %copy-done, bf16[1536]{0:T(1024)(128)(2,1)} %bout_ref.1, bf16[1536]{0:T(1024)(128)(2,1)} %scale_ref.1, bf16[1536]{0:T(1024)(128)(2,1)} %bias_ref.1, bf16[40,1536]{1,0:T(8,128)(2,1)} %bitcast.20, s32[8,64]{1,0:T(8,128)} %bitcast.23, ...), custom_call_target="tpu_custom_call" | custom-call | tf_op jit(solution)/shard_map/moe/pallas_call | solution.py:338
  64.1 0.7 %copy.23 = bf16[64,1536]{1,0:T(8,128)(2,1)} copy(bf16[64,1536]{1,0:T(8,128)(2,1)S(1)} %moe.1) | data formatting | bytes 393216
Async XLA Ops:
  19.9 0.6 copy-start

commit v3 on v2

v3 whole, which is shorter than its diff:
```python
import functools

import jax
import jax.numpy as jnp
from jax import lax
from jax.experimental import pallas as pl
from jax.experimental.pallas import tpu as pltpu
from jax.sharding import PartitionSpec as P

EPS = 1e-5
F32 = jnp.float32
BF16 = jnp.bfloat16
MESH = pl.DeviceIdType.MESH
VMEM_LIMIT = 66_400_000
MOE_LIMIT = 65_900_000
NT = (((1,), (1,)), ((), ()))
BB = 8
COLS = 6
LAG = 3
AHEAD = 3
W_PARTS = 4


def normalize(vals_f32, ln_scale, ln_bias):
    row_mean = jnp.mean(vals_f32, axis=-1, keepdims=True)
    centered = vals_f32 - row_mean
    row_var = jnp.mean(centered * centered, axis=-1, keepdims=True)
    normed = centered * lax.rsqrt(row_var + EPS)
    return (normed * ln_scale + ln_bias).astype(BF16)


def row_of(vec_ref):
    return vec_ref[...].astype(F32)[None, :]


def attention_kernel(lens_hbm, hid_hbm, cos_hbm, sin_hbm, scale_hbm, bias_hbm, bqkv_hbm, wqkv_hbm, wout_hbm, k_hbm, v_hbm,
                     part_ref, ko_hbm, vo_hbm, lens_ref, hid_ref, cos_ref, sin_ref, scale_ref, bias_ref, bqkv_ref,
                     k_buf, v_buf, w_buf, wo_buf, q_buf, kn_buf, vn_buf, c_buf, in_sem, w_sem, wo_sem, k_sem, v_sem, ko_sem, vo_sem):
    n_rows = hid_ref.shape[0]
    n_blocks = n_rows // BB
    s_max = k_buf.shape[2]
    smalls = ((hid_hbm, hid_ref), (scale_hbm, scale_ref), (bias_hbm, bias_ref), (bqkv_hbm, bqkv_ref), (cos_hbm, cos_ref), (sin_hbm, sin_ref),
              (lens_hbm, lens_ref))
    small_copies = [pltpu.make_async_copy(src, dst, in_sem.at[i]) for i, (src, dst) in enumerate(smalls)]
    w_rows = w_buf.shape[0] // W_PARTS
    w_copies = [pltpu.make_async_copy(wqkv_hbm.at[pl.ds(i * w_rows, w_rows)], w_buf.at[pl.ds(i * w_rows, w_rows)], w_sem.at[i]) for i in range(W_PARTS)]
    wo_copy = pltpu.make_async_copy(wout_hbm, wo_buf, wo_sem)
    for copy in small_copies[:3] + w_copies + small_copies[3:]:
        copy.start()

    def fetch(i):
        rows = pl.ds(i * BB, BB)
        return (pltpu.make_async_copy(k_hbm.at[rows], k_buf.at[rows], k_sem.at[i]),
                pltpu.make_async_copy(v_hbm.at[rows], v_buf.at[rows], v_sem.at[i]))

    def flush(i):
        rows = pl.ds(i * BB, BB)
        return (pltpu.make_async_copy(k_buf.at[rows], ko_hbm.at[rows], ko_sem.at[i]),
                pltpu.make_async_copy(v_buf.at[rows], vo_hbm.at[rows], vo_sem.at[i]))

    def fetch_start(i):
        for copy in fetch(i):
            copy.start()

    for i in range(AHEAD):
        fetch_start(i)

    for copy in small_copies:
        copy.wait()
    normed = normalize(hid_ref[...].astype(F32), row_of(scale_ref), row_of(bias_ref))
    for copy in w_copies:
        copy.wait()
    fetch_start(AHEAD)
    qkv = jnp.dot(normed, w_buf[...], preferred_element_type=F32) + row_of(bqkv_ref)
    qkv = qkv.astype(BF16).astype(F32)
    qkv = jnp.concatenate([qkv, jnp.zeros((128 - n_rows, qkv.shape[1]), F32)], axis=0)
    feats = qkv.T
    cos_t = jnp.concatenate([cos_ref[...], jnp.zeros((32, 128 - n_rows), F32)], axis=1)
    sin_t = jnp.concatenate([sin_ref[...], jnp.zeros((32, 128 - n_rows), F32)], axis=1)

    def rotate(base):
        u, w = feats[base:base + 32], feats[base + 32:base + 64]
        return jnp.concatenate([u * cos_t - w * sin_t, w * cos_t + u * sin_t], axis=0).astype(BF16).astype(F32)

    zeros = jnp.zeros((64, 128), F32)
    for g in range(2):
        for j in range(3):
            q_rot = rotate(g * 320 + j * 64)
            both = jnp.concatenate([q_rot, zeros] if g == 0 else [zeros, q_rot], axis=0)
            q_buf[pl.ds(g * 3 + j, n_rows, stride=8), :] = both.T[:n_rows]
    for r in (6, 7):
        q_buf[pl.ds(r, n_rows, stride=8), :] = jnp.zeros((n_rows, 128), F32)
    k_new = jnp.concatenate([rotate(192), rotate(320 + 192)], axis=0)
    v_new = jnp.concatenate([feats[256:320], feats[320 + 256:320 + 320]], axis=0)
    for i in range(n_blocks):
        kn_buf[i] = k_new if i == 0 else pltpu.roll(k_new, 128 - i * BB, 1)
        vn_buf[i] = v_new if i == 0 else pltpu.roll(v_new, 128 - i * BB, 1)

    def block(i, carry):
        for copy in fetch(i):
            copy.wait()

        @pl.when(i + AHEAD + 1 < n_blocks)
        def _():
            fetch_start(i + AHEAD + 1)

        @pl.when(i == n_blocks - AHEAD - 1)
        def _():
            wo_copy.start()

        k_cols, v_cols = kn_buf[i], vn_buf[i]
        lane = lax.broadcasted_iota(jnp.int32, (128, 128), 1)
        position = lax.broadcasted_iota(jnp.int32, (8, s_max), 1)
        scores = []
        for j in range(BB):
            b = i * BB + j
            pos = lens_ref[b]
            first = pl.multiple_of((pos // 128) * 128, 128)
            hit = lane == pos - first
            window = pl.ds(first, 128)
            k_buf[b, :, window] = jnp.where(hit, k_cols[:, j:j + 1], k_buf[b, :, window].astype(F32)).astype(BF16)
            v_buf[b, :, window] = jnp.where(hit, v_cols[:, j:j + 1], v_buf[b, :, window].astype(F32)).astype(BF16)
            rows = pl.ds(pl.multiple_of(b * 8, 8), 8)
            one = jnp.dot(q_buf[rows, :].astype(BF16), k_buf[b], preferred_element_type=F32) * 0.125
            scores.append(jnp.where(position <= pos, one, -jnp.inf))
        scores = jnp.concatenate(scores, axis=0)
        top = jnp.max(scores, axis=1, keepdims=True)
        weights = jnp.exp(scores - top)
        probs = weights * (1.0 / jnp.sum(weights, axis=1, keepdims=True))
        for j in range(BB):
            b = i * BB + j
            rows = pl.ds(pl.multiple_of(b * 8, 8), 8)
            c_buf[rows, :] = lax.dot_general(probs[j * 8:j * 8 + 8].astype(BF16), v_buf[b], NT, preferred_element_type=F32)
        for copy in flush(i):
            copy.start()
        return carry

    lax.fori_loop(0, n_blocks, block, 0)
    heads = [c_buf[pl.ds(r, n_rows, stride=8), :] for r in range(6)]
    low = lax.broadcasted_iota(jnp.int32, (n_rows, 128), 1) < 64
    ctx = jnp.concatenate([
        jnp.where(low, heads[0], pltpu.roll(heads[1], 64, 1)),
        jnp.where(low, heads[2], heads[3]),
        jnp.where(low, pltpu.roll(heads[4], 64, 1), heads[5]),
    ], axis=1).astype(BF16)
    wo_copy.wait()
    part_ref[...] = jnp.dot(ctx, wo_buf[...], preferred_element_type=F32).astype(BF16)
    for i in range(n_blocks):
        for copy in flush(i):
            copy.wait()


def moe_kernel(hid_ref, part_ref, bout_ref, scale_ref, bias_ref, wr_ref, ids_ref, wg_hbm, wu_hbm, wd_hbm, out_ref,
               wgu, wd, wr, part, from_end, pair, across_in, x1, h2, ids_buf, act, lo, hi, d_recv, y_send, y_recv,
               t_part, t_end, t_pair, t_across, o_buf, wsem, ssem, rsem):
    z, ep = lax.axis_index("tp"), lax.axis_index("ep")
    n_rows, d_model = hid_ref.shape
    n_exp = wgu.shape[0]
    width = d_model // COLS
    n_pieces = n_rows // 16
    near = z + 1 - 2 * lax.rem(z, 2)
    across = 3 - z
    y_peer = lax.rem(ep + 2, 4)
    partner = ep + 1 - 2 * lax.rem(ep, 2)
    diagonal = 3 - ep
    is_mid = jnp.logical_or(z == 1, z == 2)
    is_end = jnp.logical_or(z == 0, z == 3)
    barrier = pltpu.get_barrier_semaphore()
    pl.semaphore_signal(barrier, inc=1, device_id={"tp": near}, device_id_type=MESH)
    for peer in (y_peer, partner, diagonal):
        pl.semaphore_signal(barrier, inc=1, device_id={"ep": peer}, device_id_type=MESH)

    @pl.when(is_mid)
    def _():
        pl.semaphore_signal(barrier, inc=1, device_id={"tp": across}, device_id_type=MESH)

    loads = []
    for e in range(n_exp):
        loads.append(pltpu.make_async_copy(wg_hbm.at[e], wgu.at[e, :, 0:128], wsem.at[2 * e]))
        loads.append(pltpu.make_async_copy(wu_hbm.at[e], wgu.at[e, :, 128:256], wsem.at[2 * e + 1]))
    loads.append(pltpu.make_async_copy(wd_hbm, wd, wsem.at[2 * n_exp]))
    for load in loads:
        load.start()

    part[...] = part_ref[...]
    ids_buf[0] = ids_ref[...]
    wr[...] = jnp.concatenate([wr_ref[...], jnp.zeros((128 - wr_ref.shape[0], d_model), BF16)], axis=0)

    count = [0]

    def slots(n):
        count[0] += n
        return list(range(count[0] - n, count[0]))

    def remote(src, dst, slot, device):
        return pltpu.make_async_remote_copy(src_ref=src, dst_ref=dst, send_sem=ssem.at[slot], recv_sem=rsem.at[slot],
                                            device_id=device, device_id_type=MESH)

    def rows(k, shard=0):
        return pl.ds(shard * n_rows + k * 16, 16)

    def cols(n):
        return pl.ds(n * width, width)

    s_a, s_b, s_c, s_y, s_p, s_pp = (slots(n_pieces) for _ in range(6))
    s_ids = slots(3)
    s_d, s_yy, s_e, s_f, s_g = (slots(COLS) for _ in range(5))
    pieces = range(n_pieces)
    a = [remote(part.at[rows(k)], from_end.at[rows(k)], s_a[k], {"tp": near}) for k in pieces]
    b = [remote(pair.at[rows(k)], across_in.at[rows(k)], s_b[k], {"tp": across}) for k in pieces]
    c = [remote(x1.at[rows(k)], x1.at[rows(k)], s_c[k], {"tp": near}) for k in pieces]
    to_y = [remote(h2.at[rows(k)], h2.at[rows(k, 1)], s_y[k], {"ep": y_peer}) for k in pieces]
    to_p = [remote(h2.at[rows(k)], h2.at[rows(k, 2)], s_p[k], {"ep": partner}) for k in pieces]
    y_to_p = [remote(h2.at[rows(k, 1)], h2.at[rows(k, 3)], s_pp[k], {"ep": partner}) for k in pieces]
    to_ids = [remote(ids_ref, ids_buf.at[i + 1], s_ids[i], {"ep": peer}) for i, peer in enumerate((y_peer, partner, diagonal))]
    chunks = range(COLS)
    to_d = [remote(hi.at[:, cols(n)], d_recv.at[:, cols(n)], s_d[n], {"ep": partner}) for n in chunks]
    to_yy = [remote(y_send.at[:, cols(n)], y_recv.at[:, cols(n)], s_yy[n], {"ep": y_peer}) for n in chunks]
    to_mid = [remote(t_part.at[:, cols(n)], t_end.at[:, cols(n)], s_e[n], {"tp": near}) for n in chunks]
    to_mate = [remote(t_pair.at[:, cols(n)], t_across.at[:, cols(n)], s_f[n], {"tp": across}) for n in chunks]
    to_end = [remote(o_buf.at[:, cols(n)], o_buf.at[:, cols(n)], s_g[n], {"tp": near}) for n in chunks]

    @pl.when(is_end)
    def _():
        pl.semaphore_wait(barrier, 4)
        for k in pieces:
            a[k].start()

    @pl.when(is_mid)
    def _():
        pl.semaphore_wait(barrier, 5)

    for copy in to_ids:
        copy.start()

    @pl.when(is_mid)
    def _():
        for k in pieces:
            a[k].wait_recv()
            pair[rows(k), :] = (part[rows(k), :].astype(F32) + from_end[rows(k), :].astype(F32)).astype(BF16)
            b[k].start()

    scale, bias, bout = row_of(scale_ref), row_of(bias_ref), row_of(bout_ref)
    for k in pieces:
        @pl.when(is_mid)
        def _():
            b[k].wait_recv()
            total = pair[rows(k), :].astype(F32) + across_in[rows(k), :].astype(F32)
            x1[rows(k), :] = (hid_ref[rows(k), :].astype(F32) + total + bout).astype(BF16)
            c[k].start()

        @pl.when(is_end)
        def _():
            c[k].wait_recv()

        h2[rows(k), :] = normalize(x1[rows(k), :].astype(F32), scale, bias)
        to_y[k].start()
        to_p[k].start()

    def masks(shard):
        picks = ids_buf[shard]
        expert = lax.broadcasted_iota(jnp.int32, (128, n_rows), 0)
        hit = jnp.zeros((128, n_rows), F32)
        for k in range(picks.shape[0]):
            hit = jnp.where(expert == picks[k:k + 1, :], 1.0, hit)
        return hit.T

    def up(shard):
        toks = h2[shard * n_rows:(shard + 1) * n_rows, :]
        logits = lax.dot_general(toks, wr[...], NT, preferred_element_type=F32)
        logits = jnp.where(masks(shard) > 0.5, logits, -jnp.inf)
        shifted = jnp.exp(logits - jnp.max(logits, axis=1, keepdims=True))
        gates = (shifted / jnp.sum(shifted, axis=1, keepdims=True)).astype(BF16).astype(F32)
        gates = pltpu.roll(gates, lax.rem(128 - ep * n_exp, 128), 1)
        for e in range(n_exp):
            if shard == 0:
                loads[2 * e].wait()
                loads[2 * e + 1].wait()
            pre = jnp.dot(toks, wgu[e], preferred_element_type=F32)
            gate_pre, up_pre = pre[:, :128], pre[:, 128:]
            hidden = (gate_pre * jax.nn.sigmoid(gate_pre) * up_pre).astype(BF16).astype(F32)
            act[shard * n_rows:(shard + 1) * n_rows, e * 128:(e + 1) * 128] = (hidden * gates[:, e:e + 1]).astype(BF16)

    def relay(k):
        to_y[k].wait_recv()
        y_to_p[k].start()

    for k in (0, 1):
        relay(k)
    up(0)
    for k in (2, 3):
        relay(k)
    for copy in to_p + to_ids:
        copy.wait_recv()
    up(2)
    up(1)
    for copy in y_to_p:
        copy.wait_recv()
    up(3)
    loads[-1].wait()

    def reduce_pair(n):
        to_d[n].wait_recv()
        y_send[:, cols(n)] = (lo[64:128, cols(n)] + d_recv[64:128, cols(n)].astype(F32)).astype(BF16)
        to_yy[n].start()

    for n in chunks:
        hi[:, cols(n)] = jnp.dot(act[128:256, :], wd[:, cols(n)], preferred_element_type=F32).astype(BF16)
        to_d[n].start()
        lo[:, cols(n)] = jnp.dot(act[0:128, :], wd[:, cols(n)], preferred_element_type=F32)
        if n >= LAG:
            reduce_pair(n - LAG)
    for n in range(COLS - LAG, COLS):
        reduce_pair(n)

    def own_sum(n):
        to_yy[n].wait_recv()
        return lo[0:64, cols(n)] + d_recv[0:64, cols(n)].astype(F32) + y_recv[:, cols(n)].astype(F32)

    @pl.when(is_end)
    def _():
        for n in chunks:
            t_part[:, cols(n)] = own_sum(n).astype(BF16)
            to_mid[n].start()
        for n in chunks:
            to_end[n].wait_recv()

    @pl.when(is_mid)
    def _():
        for n in chunks:
            mine = own_sum(n)
            to_mid[n].wait_recv()
            t_pair[:, cols(n)] = (mine + t_end[:, cols(n)].astype(F32)).astype(BF16)
            to_mate[n].start()
        for n in chunks:
            to_mate[n].wait_recv()
            moe = t_pair[:, cols(n)].astype(F32) + t_across[:, cols(n)].astype(F32)
            o_buf[:, cols(n)] = (x1[:, cols(n)].astype(F32) + moe).astype(BF16)
            to_end[n].start()

    out_ref[...] = o_buf[...]
    for copy in to_y + to_p + y_to_p + to_ids + to_d + to_yy:
        copy.wait_send()

    @pl.when(is_end)
    def _():
        for copy in a + to_mid:
            copy.wait_send()

    @pl.when(is_mid)
    def _():
        for copy in b + c + to_mate + to_end:
            copy.wait_send()


N_SLOTS = 6 * 4 + 3 + 5 * COLS


def solution(mesh):
    token_rows = P(('dp', 'ep'), None)
    token_vec = P(('dp', 'ep'))
    cache_spec = P(('dp', 'ep'), None, 'tp', None)
    expert_in = P('ep', None, 'tp')
    expert_down = P('ep', 'tp', None)
    vm = pl.BlockSpec(memory_space=pltpu.VMEM)
    anyspace = pl.BlockSpec(memory_space=pl.ANY)

    def device_step(hidden, seq_lens, rope_cos, rope_sin, ln1_scale, ln1_bias, w_qkv, b_qkv, w_out, b_out, k_cache, v_cache, ln2_scale, ln2_bias, w_router, expert_ids, w_gate, w_up, w_down):
        n, d = hidden.shape
        _, s_max, groups, head = k_cache.shape
        feat = groups * head
        n_exp = w_gate.shape[0]
        k_in = k_cache.transpose(0, 2, 3, 1).reshape(n, feat, s_max)
        v_in = v_cache.transpose(0, 2, 3, 1).reshape(n, feat, s_max)
        part, k_out, v_out = pl.pallas_call(
            attention_kernel,
            out_shape=(pltpu.VMEM((n, d), BF16), jax.ShapeDtypeStruct(k_in.shape, BF16), jax.ShapeDtypeStruct(v_in.shape, BF16)),
            in_specs=[anyspace] * 11,
            out_specs=(vm, anyspace, anyspace),
            scratch_shapes=[
                pltpu.SMEM((n,), jnp.int32), pltpu.VMEM((n, d), BF16), pltpu.VMEM((32, n), F32), pltpu.VMEM((32, n), F32),
                pltpu.VMEM((d,), BF16), pltpu.VMEM((d,), BF16), pltpu.VMEM(b_qkv.shape, BF16),
                pltpu.VMEM(k_in.shape, BF16), pltpu.VMEM(v_in.shape, BF16), pltpu.VMEM(w_qkv.shape, BF16), pltpu.VMEM(w_out.shape, BF16),
                pltpu.VMEM((n * 8, 128), F32), pltpu.VMEM((n // BB, 128, 128), F32), pltpu.VMEM((n // BB, 128, 128), F32), pltpu.VMEM((n * 8, 128), F32),
                pltpu.SemaphoreType.DMA((7,)), pltpu.SemaphoreType.DMA((W_PARTS,)), pltpu.SemaphoreType.DMA, pltpu.SemaphoreType.DMA((n // BB,)), pltpu.SemaphoreType.DMA((n // BB,)),
                pltpu.SemaphoreType.DMA((n // BB,)), pltpu.SemaphoreType.DMA((n // BB,)),
            ],
            compiler_params=pltpu.CompilerParams(vmem_limit_bytes=VMEM_LIMIT),
            name="attention",
        )(seq_lens, hidden, rope_cos.T, rope_sin.T, ln1_scale, ln1_bias, b_qkv, w_qkv, w_out, k_in, v_in)
        part = pltpu.with_memory_space_constraint(part, pltpu.VMEM)
        rows = lambda r, t: pltpu.VMEM((r, d), t)
        hidden_out = pl.pallas_call(
            moe_kernel,
            out_shape=pltpu.VMEM((n, d), BF16),
            in_specs=[vm] * 7 + [anyspace] * 3,
            out_specs=vm,
            scratch_shapes=[
                pltpu.VMEM((n_exp, d, 256), BF16), pltpu.VMEM((n_exp * 128, d), BF16), rows(128, BF16),
                rows(64, BF16), rows(64, BF16), rows(64, BF16), rows(64, BF16), rows(64, BF16), rows(256, BF16), pltpu.VMEM((4, 8, n), jnp.int32),
                pltpu.VMEM((256, n_exp * 128), BF16), rows(128, F32), rows(128, BF16), rows(128, BF16), rows(64, BF16), rows(64, BF16),
                rows(64, BF16), rows(64, BF16), rows(64, BF16), rows(64, BF16), rows(64, BF16),
                pltpu.SemaphoreType.DMA((2 * n_exp + 1,)), pltpu.SemaphoreType.DMA((N_SLOTS,)), pltpu.SemaphoreType.DMA((N_SLOTS,)),
            ],
            compiler_params=pltpu.CompilerParams(vmem_limit_bytes=MOE_LIMIT, collective_id=0, has_side_effects=True),
            name="moe",
        )(hidden, part, b_out, ln2_scale, ln2_bias, w_router.T, expert_ids.T, w_gate, w_up, w_down.reshape(n_exp * 128, d))
        unfold = lambda c: c.reshape(n, groups, head, s_max).transpose(0, 3, 1, 2)
        return hidden_out, unfold(k_out), unfold(v_out)

    in_specs = (token_rows, token_vec, token_rows, token_rows, P(), P(), P(None, 'tp'), P('tp'), P('tp', None), P(), cache_spec, cache_spec, P(), P(), P(), token_rows, expert_in, expert_in, expert_down)
    return jax.shard_map(device_step, mesh=mesh, in_specs=in_specs, out_specs=(token_rows, cache_spec, cache_spec), check_vma=False)
```

time: 64.9 us -> 62.2 us (0.958)
  Pallas kernels: 62.8 us -> 60.7 us
    pallas_call x1, Pallas kernels: 19.2 us -> 13.6 us  [device_step(): pl.pallas_call(attention_kernel, out_shape=(pltpu.VMEM((n, d), BF16), jax...]
    pallas_call x1, Pallas kernels: 43.6 us -> 47.1 us  [device_step(): pl.pallas_call(moe_kernel, out_shape=pltpu.VMEM((n, d), BF16), in_specs=[...]
where the time goes in v3:
time: 62.2 us; the launch traced here: 62 us
  Pallas kernels  60.7 us (98%)
  local copies, waits for them, and re-layouts  0.68 us (1%)
  between operations  0.65 us (1%)
    pallas_call x1, Pallas kernels, device_step(): pl.pallas_call(moe_kernel, out_shape=pltpu.VMEM((n, d), BF16), in_specs=[...  47.1 us
    pallas_call x1, Pallas kernels, device_step(): pl.pallas_call(attention_kernel, out_shape=(pltpu.VMEM((n, d), BF16), jax...  13.6 us

profile of v3, /device:TPU:0, one launch (start us, length us, event | category | flops | bytes accessed | tf_op | source)
XLA Modules:
  0.0 62.0 jit_solution(6598664185752397117)
XLA Ops:
  0.6 13.6 %attention.1 = (bf16[64,1536]{1,0:T(8,128)(2,1)S(1)}, bf16[64,128,512]{2,1,0:T(8,128)(2,1)}, bf16[64,128,512]{2,1,0:T(8,128)(2,1)}) custom-call(s32[64]{0:T(128)} %lens_hbm.1, bf16[64,1536]{1,0:T(8,128)(2,1)} %hid_ref.1, f32[32,64]{1,0:T(8,128)} %bitcast.21, f32[32,64]{1,0:T(8,128)} %bitcast.22, bf16[1536]{0:T(1024)(128)(2,1)} %scale_hbm.1, ...), custom_call_target="tpu_custom_call" | custom-call | tf_op jit(solution)/shard_map/attention/pallas_call | solution.py:375
  14.2 47.1 %moe.1 = bf16[64,1536]{1,0:T(8,128)(2,1)S(1)} custom-call(bf16[64,1536]{1,0:T(8,128)(2,1)} %hid_ref.1, bf16[64,1536]{1,0:T(8,128)(2,1)S(1)} %get-tuple-element.6.part_ref, bf16[1536]{0:T(1024)(128)(2,1)} %bout_ref.1, bf16[1536]{0:T(1024)(128)(2,1)} %scale_ref.1, bf16[1536]{0:T(1024)(128)(2,1)} %bias_ref.1, bf16[40,1536]{1,0:T(8,128)(2,1)} %bitcast.20, ...), custom_call_target="tpu_custom_call" | custom-call | tf_op jit(solution)/shard_map/moe/pallas_call | solution.py:393
  61.4 0.7 %copy.23 = bf16[64,1536]{1,0:T(8,128)(2,1)} copy(bf16[64,1536]{1,0:T(8,128)(2,1)S(1)} %moe.1) | data formatting | bytes 393216

commit v4 on v2

--- a/solution.py
+++ b/solution.py
@@ -11,11 +11,13 @@
 F32 = jnp.float32
 BF16 = jnp.bfloat16
 MESH = pl.DeviceIdType.MESH
-VMEM_LIMIT = 66_600_000
-MOE_LIMIT = 66_200_000
+VMEM_LIMIT = 66_400_000
+MOE_LIMIT = 64_500_000
 NT = (((1,), (1,)), ((), ()))
 BB = 8
 COLS = 3
+AHEAD = 3
+W_PARTS = 4
 
 
 def normalize(vals_f32, ln_scale, ln_bias):
@@ -30,17 +32,19 @@
     return vec_ref[...].astype(F32)[None, :]
 
 
-def attention_kernel(lens_hbm, hid_hbm, cos_hbm, sin_hbm, scale_hbm, bias_hbm, bqkv_hbm, wqkv_hbm, k_hbm, v_hbm,
-                     ctx_ref, ko_hbm, vo_hbm, lens_ref, hid_ref, cos_ref, sin_ref, scale_ref, bias_ref, bqkv_ref,
-                     k_buf, v_buf, w_buf, q_buf, kn_buf, vn_buf, c_buf, in_sem, w_sem, k_sem, v_sem, ko_sem, vo_sem):
+def attention_kernel(lens_hbm, hid_hbm, cos_hbm, sin_hbm, scale_hbm, bias_hbm, bqkv_hbm, wqkv_hbm, wout_hbm, k_hbm, v_hbm,
+                     part_ref, ko_hbm, vo_hbm, lens_ref, hid_ref, cos_ref, sin_ref, scale_ref, bias_ref, bqkv_ref,
+                     k_buf, v_buf, w_buf, wo_buf, q_buf, kn_buf, vn_buf, c_buf, in_sem, w_sem, wo_sem, k_sem, v_sem, ko_sem, vo_sem):
     n_rows = hid_ref.shape[0]
     n_blocks = n_rows // BB
     s_max = k_buf.shape[2]
     smalls = ((hid_hbm, hid_ref), (scale_hbm, scale_ref), (bias_hbm, bias_ref), (bqkv_hbm, bqkv_ref), (cos_hbm, cos_ref), (sin_hbm, sin_ref),
               (lens_hbm, lens_ref))
     small_copies = [pltpu.make_async_copy(src, dst, in_sem.at[i]) for i, (src, dst) in enumerate(smalls)]
-    w_copy = pltpu.make_async_copy(wqkv_hbm, w_buf, w_sem)
-    for copy in small_copies[:3] + [w_copy] + small_copies[3:]:
+    w_rows = w_buf.shape[0] // W_PARTS
+    w_copies = [pltpu.make_async_copy(wqkv_hbm.at[pl.ds(i * w_rows, w_rows)], w_buf.at[pl.ds(i * w_rows, w_rows)], w_sem.at[i]) for i in range(W_PARTS)]
+    wo_copy = pltpu.make_async_copy(wout_hbm, wo_buf, wo_sem)
+    for copy in small_copies[:3] + w_copies + small_copies[3:]:
         copy.start()
 
     def fetch(i):
@@ -53,14 +57,19 @@
         return (pltpu.make_async_copy(k_buf.at[rows], ko_hbm.at[rows], ko_sem.at[i]),
                 pltpu.make_async_copy(v_buf.at[rows], vo_hbm.at[rows], vo_sem.at[i]))
 
-    for i in range(n_blocks):
+    def fetch_start(i):
         for copy in fetch(i):
             copy.start()
+
+    for i in range(AHEAD):
+        fetch_start(i)
 
     for copy in small_copies:
         copy.wait()
     normed = normalize(hid_ref[...].astype(F32), row_of(scale_ref), row_of(bias_ref))
-    w_copy.wait()
+    for copy in w_copies:
+        copy.wait()
+    fetch_start(AHEAD)
     qkv = jnp.dot(normed, w_buf[...], preferred_element_type=F32) + row_of(bqkv_ref)
     qkv = qkv.astype(BF16).astype(F32)
     qkv = jnp.concatenate([qkv, jnp.zeros((128 - n_rows, qkv.shape[1]), F32)], axis=0)
@@ -89,6 +98,15 @@
     def block(i, carry):
         for copy in fetch(i):
             copy.wait()
+
+        @pl.when(i + AHEAD + 1 < n_blocks)
+        def _():
+            fetch_start(i + AHEAD + 1)
+
+        @pl.when(i == n_blocks - AHEAD - 1)
+        def _():
+            wo_copy.start()
+
         k_cols, v_cols = kn_buf[i], vn_buf[i]
         lane = lax.broadcasted_iota(jnp.int32, (128, 128), 1)
         position = lax.broadcasted_iota(jnp.int32, (8, s_max), 1)
@@ -112,24 +130,27 @@
             b = i * BB + j
             rows = pl.ds(pl.multiple_of(b * 8, 8), 8)
             c_buf[rows, :] = lax.dot_general(probs[j * 8:j * 8 + 8].astype(BF16), v_buf[b], NT, preferred_element_type=F32)
-        return carry
-
-    lax.fori_loop(0, n_blocks, block, 0)
-    for i in range(n_blocks):
         for copy in flush(i):
             copy.start()
+        return carry
+
+    lax.fori_loop(0, n_blocks, block, 0)
     heads = [c_buf[pl.ds(r, n_rows, stride=8), :] for r in range(6)]
     low = lax.broadcasted_iota(jnp.int32, (n_rows, 128), 1) < 64
-    ctx_ref[:, 0:128] = jnp.where(low, heads[0], pltpu.roll(heads[1], 64, 1)).astype(BF16)
-    ctx_ref[:, 128:256] = jnp.where(low, heads[2], heads[3]).astype(BF16)
-    ctx_ref[:, 256:384] = jnp.where(low, pltpu.roll(heads[4], 64, 1), heads[5]).astype(BF16)
+    ctx = jnp.concatenate([
+        jnp.where(low, heads[0], pltpu.roll(heads[1], 64, 1)),
+        jnp.where(low, heads[2], heads[3]),
+        jnp.where(low, pltpu.roll(heads[4], 64, 1), heads[5]),
+    ], axis=1).astype(BF16)
+    wo_copy.wait()
+    part_ref[...] = jnp.dot(ctx, wo_buf[...], preferred_element_type=F32).astype(BF16)
     for i in range(n_blocks):
         for copy in flush(i):
             copy.wait()
 
 
-def moe_kernel(hid_ref, ctx_ref, bout_ref, scale_ref, bias_ref, wr_ref, ids_ref, wout_hbm, wg_hbm, wu_hbm, wd_hbm, out_ref,
-               wout, wgu, wd, wr, part_f, part_b, rs_recv, x1_buf, h2, ids_buf, act, lo, hi, d_recv, y_send, y_recv, t_f, t_b, z_recv, o_buf,
+def moe_kernel(hid_ref, part_ref, bout_ref, scale_ref, bias_ref, wr_ref, ids_ref, wg_hbm, wu_hbm, wd_hbm, out_ref,
+               wgu, wd, wr, rs_recv, x1_buf, h2, ids_buf, act, lo, hi, d_recv, y_send, y_recv, t_f, t_b, z_recv, o_buf,
                wsem, ssem, rsem):
     z, ep = lax.axis_index("tp"), lax.axis_index("ep")
     n_rows, d_model = hid_ref.shape
@@ -145,12 +166,12 @@
     for peer in (y_peer, partner, diagonal):
         pl.semaphore_signal(barrier, inc=1, device_id={"ep": peer}, device_id_type=MESH)
 
-    loads = [pltpu.make_async_copy(wout_hbm, wout, wsem.at[0])]
+    loads = [None]
     for e in range(n_exp):
         loads.append(pltpu.make_async_copy(wg_hbm.at[e], wgu.at[e, :, 0:128], wsem.at[1 + 2 * e]))
         loads.append(pltpu.make_async_copy(wu_hbm.at[e], wgu.at[e, :, 128:256], wsem.at[2 + 2 * e]))
     loads.append(pltpu.make_async_copy(wd_hbm, wd, wsem.at[1 + 2 * n_exp]))
-    for load in loads:
+    for load in loads[1:]:
         load.start()
 
     sent = []
@@ -162,10 +183,6 @@
         sent.append(copy)
         return copy
 
-    loads[0].wait()
-    part = jnp.dot(ctx_ref[...], wout[...], preferred_element_type=F32)
-    part_f[...] = part
-    part_b[...] = part.astype(BF16)
     wr[...] = jnp.concatenate([wr_ref[...], jnp.zeros((128 - wr_ref.shape[0], d_model), BF16)], axis=0)
     ids_buf[0] = ids_ref[...]
     pl.semaphore_wait(barrier, 6)
@@ -177,7 +194,7 @@
     slot = 0
     rs = []
     for dz in range(3):
-        rs.append(send(part_b.at[rows_of(z_peers[dz])], rs_recv.at[dz], slot, {"tp": z_peers[dz]}))
+        rs.append(send(part_ref.at[rows_of(z_peers[dz])], rs_recv.at[dz], slot, {"tp": z_peers[dz]}))
         slot += 1
     id_copies = []
     for shard, peer in ((1, y_peer), (2, partner), (3, diagonal)):
@@ -185,7 +202,7 @@
         slot += 1
     for copy in rs:
         copy.wait_recv()
-    total = part_f[mine, :] + rs_recv[0].astype(F32) + rs_recv[1].astype(F32) + rs_recv[2].astype(F32)
+    total = part_ref[mine, :].astype(F32) + rs_recv[0].astype(F32) + rs_recv[1].astype(F32) + rs_recv[2].astype(F32)
     x1 = (hid_ref[mine, :].astype(F32) + total + row_of(bout_ref)).astype(BF16).astype(F32)
     x1_buf[...] = x1
     h2[mine, :] = normalize(x1, row_of(scale_ref), row_of(bias_ref))
@@ -318,38 +335,39 @@
         n_exp = w_gate.shape[0]
         k_in = k_cache.transpose(0, 2, 3, 1).reshape(n, feat, s_max)
         v_in = v_cache.transpose(0, 2, 3, 1).reshape(n, feat, s_max)
-        ctx, k_out, v_out = pl.pallas_call(
+        part, k_out, v_out = pl.pallas_call(
             attention_kernel,
-            out_shape=(pltpu.VMEM((n, 384), BF16), jax.ShapeDtypeStruct(k_in.shape, BF16), jax.ShapeDtypeStruct(v_in.shape, BF16)),
-            in_specs=[anyspace] * 10,
+            out_shape=(pltpu.VMEM((n, d), BF16), jax.ShapeDtypeStruct(k_in.shape, BF16), jax.ShapeDtypeStruct(v_in.shape, BF16)),
+            in_specs=[anyspace] * 11,
             out_specs=(vm, anyspace, anyspace),
             scratch_shapes=[
                 pltpu.SMEM((n,), jnp.int32), pltpu.VMEM((n, d), BF16), pltpu.VMEM((32, n), F32), pltpu.VMEM((32, n), F32),
                 pltpu.VMEM((d,), BF16), pltpu.VMEM((d,), BF16), pltpu.VMEM(b_qkv.shape, BF16),
-                pltpu.VMEM(k_in.shape, BF16), pltpu.VMEM(v_in.shape, BF16), pltpu.VMEM(w_qkv.shape, BF16),
+                pltpu.VMEM(k_in.shape, BF16), pltpu.VMEM(v_in.shape, BF16), pltpu.VMEM(w_qkv.shape, BF16), pltpu.VMEM(w_out.shape, BF16),
                 pltpu.VMEM((n * 8, 128), F32), pltpu.VMEM((n // BB, 128, 128), F32), pltpu.VMEM((n // BB, 128, 128), F32), pltpu.VMEM((n * 8, 128), F32),
-                pltpu.SemaphoreType.DMA((7,)), pltpu.SemaphoreType.DMA, pltpu.SemaphoreType.DMA((n // BB,)), pltpu.SemaphoreType.DMA((n // BB,)),
+                pltpu.SemaphoreType.DMA((7,)), pltpu.SemaphoreType.DMA((W_PARTS,)), pltpu.SemaphoreType.DMA, pltpu.SemaphoreType.DMA((n // BB,)), pltpu.SemaphoreType.DMA((n // BB,)),
                 pltpu.SemaphoreType.DMA((n // BB,)), pltpu.SemaphoreType.DMA((n // BB,)),
             ],
             compiler_params=pltpu.CompilerParams(vmem_limit_bytes=VMEM_LIMIT),
             name="attention",
-        )(seq_lens, hidden, rope_cos.T, rope_sin.T, ln1_scale, ln1_bias, b_qkv, w_qkv, k_in, v_in)
+        )(seq_lens, hidden, rope_cos.T, rope_sin.T, ln1_scale, ln1_bias, b_qkv, w_qkv, w_out, k_in, v_in)
+        part = pltpu.with_memory_space_constraint(part, pltpu.VMEM)
         rows = lambda r, t: pltpu.VMEM((r, d), t)
         hidden_out = pl.pallas_call(
             moe_kernel,
             out_shape=pltpu.VMEM((n, d), BF16),
-            in_specs=[vm] * 7 + [anyspace] * 4,
+            in_specs=[vm] * 7 + [anyspace] * 3,
             out_specs=vm,
             scratch_shapes=[
-                pltpu.VMEM(w_out.shape, BF16), pltpu.VMEM((n_exp, d, 256), BF16), pltpu.VMEM((n_exp * 128, d), BF16), rows(128, BF16),
-                rows(64, F32), rows(64, BF16), pltpu.VMEM((3, 16, d), BF16), rows(16, F32), rows(256, BF16), pltpu.VMEM((4, 8, n), jnp.int32),
+                pltpu.VMEM((n_exp, d, 256), BF16), pltpu.VMEM((n_exp * 128, d), BF16), rows(128, BF16),
+                pltpu.VMEM((3, 16, d), BF16), rows(16, F32), rows(256, BF16), pltpu.VMEM((4, 8, n), jnp.int32),
                 pltpu.VMEM((256, n_exp * 128), BF16), rows(128, F32), rows(128, BF16), rows(128, BF16), rows(64, BF16), rows(64, BF16),
                 rows(64, F32), rows(64, BF16), pltpu.VMEM((3, 16, d), BF16), rows(64, BF16),
                 pltpu.SemaphoreType.DMA((2 * n_exp + 2,)), pltpu.SemaphoreType.DMA((N_SLOTS,)), pltpu.SemaphoreType.DMA((N_SLOTS,)),
             ],
             compiler_params=pltpu.CompilerParams(vmem_limit_bytes=MOE_LIMIT, collective_id=0, has_side_effects=True),
             name="moe",
-        )(hidden, ctx, b_out, ln2_scale, ln2_bias, w_router.T, expert_ids.T, w_out, w_gate, w_up, w_down.reshape(n_exp * 128, d))
+        )(hidden, part, b_out, ln2_scale, ln2_bias, w_router.T, expert_ids.T, w_gate, w_up, w_down.reshape(n_exp * 128, d))
         unfold = lambda c: c.reshape(n, groups, head, s_max).transpose(0, 3, 1, 2)
         return hidden_out, unfold(k_out), unfold(v_out)
 

time: 64.9 us -> 57.7 us (0.89)
  Pallas kernels: 62.8 us -> 56.2 us
    pallas_call x1, Pallas kernels: 19.2 us -> 13.6 us  [device_step(): pl.pallas_call(attention_kernel, out_shape=(pltpu.VMEM((n, d), BF16), jax...]
    pallas_call x1, Pallas kernels: 43.6 us -> 42.6 us  [device_step(): pl.pallas_call(moe_kernel, out_shape=pltpu.VMEM((n, d), BF16), in_specs=[...]
where the time goes in v4:
time: 57.7 us; the launch traced here: 57.5 us
  Pallas kernels  56.2 us (97%)
  local copies, waits for them, and re-layouts  0.68 us (1%)
  between operations  0.65 us (1%)
    pallas_call x1, Pallas kernels, device_step(): pl.pallas_call(moe_kernel, out_shape=pltpu.VMEM((n, d), BF16), in_specs=[...  42.6 us
    pallas_call x1, Pallas kernels, device_step(): pl.pallas_call(attention_kernel, out_shape=(pltpu.VMEM((n, d), BF16), jax...  13.6 us

profile of v4, /device:TPU:0, one launch (start us, length us, event | category | flops | bytes accessed | tf_op | source)
XLA Modules:
  0.0 57.5 jit_solution(517478116531728052)
XLA Ops:
  0.6 13.6 %attention.1 = (bf16[64,1536]{1,0:T(8,128)(2,1)S(1)}, bf16[64,128,512]{2,1,0:T(8,128)(2,1)}, bf16[64,128,512]{2,1,0:T(8,128)(2,1)}) custom-call(s32[64]{0:T(128)} %lens_hbm.1, bf16[64,1536]{1,0:T(8,128)(2,1)} %hid_ref.1, f32[32,64]{1,0:T(8,128)} %bitcast.21, f32[32,64]{1,0:T(8,128)} %bitcast.22, bf16[1536]{0:T(1024)(128)(2,1)} %scale_hbm.1, ...), custom_call_target="tpu_custom_call" | custom-call | tf_op jit(solution)/shard_map/attention/pallas_call | solution.py:338
  14.2 42.6 %moe.1 = bf16[64,1536]{1,0:T(8,128)(2,1)S(1)} custom-call(bf16[64,1536]{1,0:T(8,128)(2,1)} %hid_ref.1, bf16[64,1536]{1,0:T(8,128)(2,1)S(1)} %get-tuple-element.6.part_ref, bf16[1536]{0:T(1024)(128)(2,1)} %bout_ref.1, bf16[1536]{0:T(1024)(128)(2,1)} %scale_ref.1, bf16[1536]{0:T(1024)(128)(2,1)} %bias_ref.1, bf16[40,1536]{1,0:T(8,128)(2,1)} %bitcast.20, ...), custom_call_target="tpu_custom_call" | custom-call | tf_op jit(solution)/shard_map/moe/pallas_call | solution.py:356
  56.8 0.7 %copy.23 = bf16[64,1536]{1,0:T(8,128)(2,1)} copy(bf16[64,1536]{1,0:T(8,128)(2,1)S(1)} %moe.1) | data formatting | bytes 393216

commit v5 on v3

--- a/solution.py
+++ b/solution.py
@@ -12,11 +12,11 @@
 BF16 = jnp.bfloat16
 MESH = pl.DeviceIdType.MESH
 VMEM_LIMIT = 66_400_000
-MOE_LIMIT = 65_900_000
+MOE_LIMIT = 64_500_000
 NT = (((1,), (1,)), ((), ()))
 BB = 8
 COLS = 6
-LAG = 3
+PIECE = 8
 AHEAD = 3
 W_PARTS = 4
 
@@ -151,28 +151,24 @@
 
 
 def moe_kernel(hid_ref, part_ref, bout_ref, scale_ref, bias_ref, wr_ref, ids_ref, wg_hbm, wu_hbm, wd_hbm, out_ref,
-               wgu, wd, wr, part, from_end, pair, across_in, x1, h2, ids_buf, act, lo, hi, d_recv, y_send, y_recv,
+               wgu, wd, wr, rs_recv, x1, h2, ids_buf, act, own_p, y_p, hi0, hi1, d0, d1, y_send, y_recv,
                t_part, t_end, t_pair, t_across, o_buf, wsem, ssem, rsem):
     z, ep = lax.axis_index("tp"), lax.axis_index("ep")
     n_rows, d_model = hid_ref.shape
     n_exp = wgu.shape[0]
     width = d_model // COLS
-    n_pieces = n_rows // 16
-    near = z + 1 - 2 * lax.rem(z, 2)
-    across = 3 - z
+    z_peers = [lax.rem(z + dz, 4) for dz in (1, 2, 3)]
+    near, across = z + 1 - 2 * lax.rem(z, 2), 3 - z
     y_peer = lax.rem(ep + 2, 4)
     partner = ep + 1 - 2 * lax.rem(ep, 2)
     diagonal = 3 - ep
     is_mid = jnp.logical_or(z == 1, z == 2)
     is_end = jnp.logical_or(z == 0, z == 3)
     barrier = pltpu.get_barrier_semaphore()
-    pl.semaphore_signal(barrier, inc=1, device_id={"tp": near}, device_id_type=MESH)
+    for peer in z_peers:
+        pl.semaphore_signal(barrier, inc=1, device_id={"tp": peer}, device_id_type=MESH)
     for peer in (y_peer, partner, diagonal):
         pl.semaphore_signal(barrier, inc=1, device_id={"ep": peer}, device_id_type=MESH)
-
-    @pl.when(is_mid)
-    def _():
-        pl.semaphore_signal(barrier, inc=1, device_id={"tp": across}, device_id_type=MESH)
 
     loads = []
     for e in range(n_exp):
@@ -182,80 +178,73 @@
     for load in loads:
         load.start()
 
-    part[...] = part_ref[...]
+    count = [0]
+
+    def remote(src, dst, device):
+        slot = count[0]
+        count[0] += 1
+        return pltpu.make_async_remote_copy(src_ref=src, dst_ref=dst, send_sem=ssem.at[slot], recv_sem=rsem.at[slot],
+                                            device_id=device, device_id_type=MESH)
+
+    def at(index, h, shard=0):
+        return pl.ds(pl.multiple_of(shard * n_rows + index * 16 + h * PIECE, PIECE), PIECE)
+
+    def cols(n):
+        return pl.ds(n * width, width)
+
+    halves = range(16 // PIECE)
+    z_order = [z] + [lax.rem(z + 4 - dz, 4) for dz in (1, 2, 3)]
+    rs = [[remote(part_ref.at[at(z_peers[dz], h)], rs_recv.at[dz, pl.ds(h * PIECE, PIECE)], {"tp": z_peers[dz]}) for dz in range(3)] for h in halves]
+    to_z = [[remote(h2.at[at(z, h)], h2.at[at(z, h)], {"tp": z_peers[dz]}) for dz in range(3)] for h in halves]
+    to_p = [[remote(h2.at[at(z_order[k], h)], h2.at[at(z_order[k], h, 1)], {"ep": partner}) for k in range(4)] for h in halves]
+    to_y = [[remote(h2.at[at(z_order[k], h)], h2.at[at(z_order[k], h, 2)], {"ep": y_peer}) for k in range(4)] for h in halves]
+    y_to_p = [[remote(h2.at[at(z_order[k], h, 2)], h2.at[at(z_order[k], h, 3)], {"ep": partner}) for k in range(4)] for h in halves]
+    mine = pl.ds(pl.multiple_of(z * 16, 16), 16)
+    x1_z = [remote(x1.at[mine], x1.at[mine], {"tp": z_peers[dz]}) for dz in range(3)]
+    to_ids = [remote(ids_ref, ids_buf.at[i + 1], {"ep": peer}) for i, peer in enumerate((partner, y_peer, diagonal))]
+    chunks = range(COLS)
+    to_d0 = remote(hi0, d0, {"ep": partner})
+    to_d = [remote(hi1.at[:, cols(n)], d1.at[:, cols(n)], {"ep": partner}) for n in chunks]
+    to_yy = [remote(y_send.at[:, cols(n)], y_recv.at[:, cols(n)], {"ep": y_peer}) for n in chunks]
+    to_mid = [remote(t_part.at[:, cols(n)], t_end.at[:, cols(n)], {"tp": near}) for n in chunks]
+    to_mate = [remote(t_pair.at[:, cols(n)], t_across.at[:, cols(n)], {"tp": across}) for n in chunks]
+    to_end = [remote(o_buf.at[:, cols(n)], o_buf.at[:, cols(n)], {"tp": near}) for n in chunks]
+
+    scale, bias, bout = row_of(scale_ref), row_of(bias_ref), row_of(bout_ref)
     ids_buf[0] = ids_ref[...]
     wr[...] = jnp.concatenate([wr_ref[...], jnp.zeros((128 - wr_ref.shape[0], d_model), BF16)], axis=0)
-
-    count = [0]
-
-    def slots(n):
-        count[0] += n
-        return list(range(count[0] - n, count[0]))
-
-    def remote(src, dst, slot, device):
-        return pltpu.make_async_remote_copy(src_ref=src, dst_ref=dst, send_sem=ssem.at[slot], recv_sem=rsem.at[slot],
-                                            device_id=device, device_id_type=MESH)
-
-    def rows(k, shard=0):
-        return pl.ds(shard * n_rows + k * 16, 16)
-
-    def cols(n):
-        return pl.ds(n * width, width)
-
-    s_a, s_b, s_c, s_y, s_p, s_pp = (slots(n_pieces) for _ in range(6))
-    s_ids = slots(3)
-    s_d, s_yy, s_e, s_f, s_g = (slots(COLS) for _ in range(5))
-    pieces = range(n_pieces)
-    a = [remote(part.at[rows(k)], from_end.at[rows(k)], s_a[k], {"tp": near}) for k in pieces]
-    b = [remote(pair.at[rows(k)], across_in.at[rows(k)], s_b[k], {"tp": across}) for k in pieces]
-    c = [remote(x1.at[rows(k)], x1.at[rows(k)], s_c[k], {"tp": near}) for k in pieces]
-    to_y = [remote(h2.at[rows(k)], h2.at[rows(k, 1)], s_y[k], {"ep": y_peer}) for k in pieces]
-    to_p = [remote(h2.at[rows(k)], h2.at[rows(k, 2)], s_p[k], {"ep": partner}) for k in pieces]
-    y_to_p = [remote(h2.at[rows(k, 1)], h2.at[rows(k, 3)], s_pp[k], {"ep": partner}) for k in pieces]
-    to_ids = [remote(ids_ref, ids_buf.at[i + 1], s_ids[i], {"ep": peer}) for i, peer in enumerate((y_peer, partner, diagonal))]
-    chunks = range(COLS)
-    to_d = [remote(hi.at[:, cols(n)], d_recv.at[:, cols(n)], s_d[n], {"ep": partner}) for n in chunks]
-    to_yy = [remote(y_send.at[:, cols(n)], y_recv.at[:, cols(n)], s_yy[n], {"ep": y_peer}) for n in chunks]
-    to_mid = [remote(t_part.at[:, cols(n)], t_end.at[:, cols(n)], s_e[n], {"tp": near}) for n in chunks]
-    to_mate = [remote(t_pair.at[:, cols(n)], t_across.at[:, cols(n)], s_f[n], {"tp": across}) for n in chunks]
-    to_end = [remote(o_buf.at[:, cols(n)], o_buf.at[:, cols(n)], s_g[n], {"tp": near}) for n in chunks]
-
-    @pl.when(is_end)
-    def _():
-        pl.semaphore_wait(barrier, 4)
-        for k in pieces:
-            a[k].start()
-
-    @pl.when(is_mid)
-    def _():
-        pl.semaphore_wait(barrier, 5)
-
+    pl.semaphore_wait(barrier, 6)
+
+    for h in halves:
+        for dz in range(3):
+            rs[h][dz].start()
     for copy in to_ids:
         copy.start()
-
-    @pl.when(is_mid)
-    def _():
-        for k in pieces:
-            a[k].wait_recv()
-            pair[rows(k), :] = (part[rows(k), :].astype(F32) + from_end[rows(k), :].astype(F32)).astype(BF16)
-            b[k].start()
-
-    scale, bias, bout = row_of(scale_ref), row_of(bias_ref), row_of(bout_ref)
-    for k in pieces:
-        @pl.when(is_mid)
-        def _():
-            b[k].wait_recv()
-            total = pair[rows(k), :].astype(F32) + across_in[rows(k), :].astype(F32)
-            x1[rows(k), :] = (hid_ref[rows(k), :].astype(F32) + total + bout).astype(BF16)
-            c[k].start()
-
-        @pl.when(is_end)
-        def _():
-            c[k].wait_recv()
-
-        h2[rows(k), :] = normalize(x1[rows(k), :].astype(F32), scale, bias)
-        to_y[k].start()
-        to_p[k].start()
+    for h in halves:
+        for dz in range(3):
+            rs[h][dz].wait_recv()
+        got = pl.ds(h * PIECE, PIECE)
+        total = part_ref[at(z, h), :].astype(F32) + rs_recv[0, got].astype(F32) + rs_recv[1, got].astype(F32) + rs_recv[2, got].astype(F32)
+        row = (hid_ref[at(z, h), :].astype(F32) + total + bout).astype(BF16)
+        x1[at(z, h), :] = row
+        h2[at(z, h), :] = normalize(row.astype(F32), scale, bias)
+        for dz in range(3):
+            to_z[h][dz].start()
+        to_y[h][0].start()
+        to_p[h][0].start()
+    for copy in x1_z:
+        copy.start()
+
+    def relay(h, k):
+        to_y[h][k].wait_recv()
+        y_to_p[h][k].start()
+
+    for h in halves:
+        for dz in range(3):
+            to_z[h][dz].wait_recv()
+            to_y[h][dz + 1].start()
+            to_p[h][dz + 1].start()
+        relay(h, 0)
 
     def masks(shard):
         picks = ids_buf[shard]
@@ -265,57 +254,71 @@
             hit = jnp.where(expert == picks[k:k + 1, :], 1.0, hit)
         return hit.T
 
-    def up(shard):
-        toks = h2[shard * n_rows:(shard + 1) * n_rows, :]
-        logits = lax.dot_general(toks, wr[...], NT, preferred_element_type=F32)
+    def toks(shard):
+        return h2[shard * n_rows:(shard + 1) * n_rows, :]
+
+    def gates_of(shard):
+        logits = lax.dot_general(toks(shard), wr[...], NT, preferred_element_type=F32)
         logits = jnp.where(masks(shard) > 0.5, logits, -jnp.inf)
         shifted = jnp.exp(logits - jnp.max(logits, axis=1, keepdims=True))
         gates = (shifted / jnp.sum(shifted, axis=1, keepdims=True)).astype(BF16).astype(F32)
-        gates = pltpu.roll(gates, lax.rem(128 - ep * n_exp, 128), 1)
-        for e in range(n_exp):
+        return pltpu.roll(gates, lax.rem(128 - ep * n_exp, 128), 1)
+
+    def up(shard, gates, first, last):
+        rows = toks(shard)
+        for e in range(first, last):
             if shard == 0:
                 loads[2 * e].wait()
                 loads[2 * e + 1].wait()
-            pre = jnp.dot(toks, wgu[e], preferred_element_type=F32)
+            pre = jnp.dot(rows, wgu[e], preferred_element_type=F32)
             gate_pre, up_pre = pre[:, :128], pre[:, 128:]
             hidden = (gate_pre * jax.nn.sigmoid(gate_pre) * up_pre).astype(BF16).astype(F32)
             act[shard * n_rows:(shard + 1) * n_rows, e * 128:(e + 1) * 128] = (hidden * gates[:, e:e + 1]).astype(BF16)
 
-    def relay(k):
-        to_y[k].wait_recv()
-        y_to_p[k].start()
-
-    for k in (0, 1):
-        relay(k)
-    up(0)
-    for k in (2, 3):
-        relay(k)
-    for copy in to_p + to_ids:
+    for copy in to_ids:
         copy.wait_recv()
-    up(2)
-    up(1)
-    for copy in y_to_p:
-        copy.wait_recv()
-    up(3)
+    gates = gates_of(0)
+    split = n_exp // len(halves)
+    for h in halves:
+        up(0, gates, h * split, (h + 1) * split)
+        for k in (1, 2, 3):
+            relay(h, k)
+    for h in halves:
+        for copy in to_p[h]:
+            copy.wait_recv()
+    up(1, gates_of(1), 0, n_exp)
     loads[-1].wait()
+    for n in range(3):
+        third = pl.ds(n * 512, 512)
+        both = jnp.dot(act[0:128, :], wd[:, third], preferred_element_type=F32)
+        own_p[:, third] = both[0:64]
+        hi0[:, third] = both[64:128].astype(BF16)
+    to_d0.start()
+    up(2, gates_of(2), 0, n_exp)
+    for h in halves:
+        for copy in y_to_p[h]:
+            copy.wait_recv()
+    up(3, gates_of(3), 0, n_exp)
 
     def reduce_pair(n):
         to_d[n].wait_recv()
-        y_send[:, cols(n)] = (lo[64:128, cols(n)] + d_recv[64:128, cols(n)].astype(F32)).astype(BF16)
+        y_send[:, cols(n)] = (y_p[:, cols(n)] + d1[:, cols(n)].astype(F32)).astype(BF16)
         to_yy[n].start()
 
     for n in chunks:
-        hi[:, cols(n)] = jnp.dot(act[128:256, :], wd[:, cols(n)], preferred_element_type=F32).astype(BF16)
+        both = jnp.dot(act[128:256, :], wd[:, cols(n)], preferred_element_type=F32)
+        y_p[:, cols(n)] = both[0:64]
+        hi1[:, cols(n)] = both[64:128].astype(BF16)
         to_d[n].start()
-        lo[:, cols(n)] = jnp.dot(act[0:128, :], wd[:, cols(n)], preferred_element_type=F32)
-        if n >= LAG:
-            reduce_pair(n - LAG)
-    for n in range(COLS - LAG, COLS):
+    to_d0.wait_recv()
+    for n in chunks:
         reduce_pair(n)
+    for copy in x1_z:
+        copy.wait_recv()
 
     def own_sum(n):
         to_yy[n].wait_recv()
-        return lo[0:64, cols(n)] + d_recv[0:64, cols(n)].astype(F32) + y_recv[:, cols(n)].astype(F32)
+        return own_p[:, cols(n)] + d0[:, cols(n)].astype(F32) + y_recv[:, cols(n)].astype(F32)
 
     @pl.when(is_end)
     def _():
@@ -328,9 +331,9 @@
     @pl.when(is_mid)
     def _():
         for n in chunks:
-            mine = own_sum(n)
+            part_sum = own_sum(n)
             to_mid[n].wait_recv()
-            t_pair[:, cols(n)] = (mine + t_end[:, cols(n)].astype(F32)).astype(BF16)
+            t_pair[:, cols(n)] = (part_sum + t_end[:, cols(n)].astype(F32)).astype(BF16)
             to_mate[n].start()
         for n in chunks:
             to_mate[n].wait_recv()
@@ -339,21 +342,22 @@
             to_end[n].start()
 
     out_ref[...] = o_buf[...]
-    for copy in to_y + to_p + y_to_p + to_ids + to_d + to_yy:
-        copy.wait_send()
+    for group in rs + to_z + to_p + to_y + y_to_p + [x1_z, to_ids, [to_d0], to_d, to_yy]:
+        for copy in group:
+            copy.wait_send()
 
     @pl.when(is_end)
     def _():
-        for copy in a + to_mid:
+        for copy in to_mid:
             copy.wait_send()
 
     @pl.when(is_mid)
     def _():
-        for copy in b + c + to_mate + to_end:
+        for copy in to_mate + to_end:
             copy.wait_send()
 
 
-N_SLOTS = 6 * 4 + 3 + 5 * COLS
+N_SLOTS = (16 // PIECE) * 18 + 3 + 3 + 1 + 5 * COLS
 
 
 def solution(mesh):
@@ -397,9 +401,9 @@
             out_specs=vm,
             scratch_shapes=[
                 pltpu.VMEM((n_exp, d, 256), BF16), pltpu.VMEM((n_exp * 128, d), BF16), rows(128, BF16),
-                rows(64, BF16), rows(64, BF16), rows(64, BF16), rows(64, BF16), rows(64, BF16), rows(256, BF16), pltpu.VMEM((4, 8, n), jnp.int32),
-                pltpu.VMEM((256, n_exp * 128), BF16), rows(128, F32), rows(128, BF16), rows(128, BF16), rows(64, BF16), rows(64, BF16),
-                rows(64, BF16), rows(64, BF16), rows(64, BF16), rows(64, BF16), rows(64, BF16),
+                pltpu.VMEM((3, 16, d), BF16), rows(64, BF16), rows(256, BF16), pltpu.VMEM((4, 8, n), jnp.int32),
+                pltpu.VMEM((256, n_exp * 128), BF16), rows(64, F32), rows(64, F32), rows(64, BF16), rows(64, BF16), rows(64, BF16), rows(64, BF16),
+                rows(64, BF16), rows(64, BF16), rows(64, BF16), rows(64, BF16), rows(64, BF16), rows(64, BF16), rows(64, BF16),
                 pltpu.SemaphoreType.DMA((2 * n_exp + 1,)), pltpu.SemaphoreType.DMA((N_SLOTS,)), pltpu.SemaphoreType.DMA((N_SLOTS,)),
             ],
             compiler_params=pltpu.CompilerParams(vmem_limit_bytes=MOE_LIMIT, collective_id=0, has_side_effects=True),

time: 62.2 us -> 62.3 us (level)
  no operation moved by 1% of the time
where the time goes in v5:
time: 62.3 us; the launch traced here: 62.2 us
  Pallas kernels  60.8 us (98%)
  local copies, waits for them, and re-layouts  0.68 us (1%)
  between operations  0.65 us (1%)
    pallas_call x1, Pallas kernels, device_step(): pl.pallas_call(moe_kernel, out_shape=pltpu.VMEM((n, d), BF16), in_specs=[...  47.3 us
    pallas_call x1, Pallas kernels, device_step(): pl.pallas_call(attention_kernel, out_shape=(pltpu.VMEM((n, d), BF16), jax...  13.6 us

profile of v5, /device:TPU:0, one launch (start us, length us, event | category | flops | bytes accessed | tf_op | source)
XLA Modules:
  0.0 62.2 jit_solution(8487637784678080998)
XLA Ops:
  0.6 13.6 %attention.1 = (bf16[64,1536]{1,0:T(8,128)(2,1)S(1)}, bf16[64,128,512]{2,1,0:T(8,128)(2,1)}, bf16[64,128,512]{2,1,0:T(8,128)(2,1)}) custom-call(s32[64]{0:T(128)} %lens_hbm.1, bf16[64,1536]{1,0:T(8,128)(2,1)} %hid_ref.1, f32[32,64]{1,0:T(8,128)} %bitcast.21, f32[32,64]{1,0:T(8,128)} %bitcast.22, bf16[1536]{0:T(1024)(128)(2,1)} %scale_hbm.1, ...), custom_call_target="tpu_custom_call" | custom-call | tf_op jit(solution)/shard_map/attention/pallas_call | solution.py:379
  14.2 47.3 %moe.1 = bf16[64,1536]{1,0:T(8,128)(2,1)S(1)} custom-call(bf16[64,1536]{1,0:T(8,128)(2,1)} %hid_ref.1, bf16[64,1536]{1,0:T(8,128)(2,1)S(1)} %get-tuple-element.6.part_ref, bf16[1536]{0:T(1024)(128)(2,1)} %bout_ref.1, bf16[1536]{0:T(1024)(128)(2,1)} %scale_ref.1, bf16[1536]{0:T(1024)(128)(2,1)} %bias_ref.1, bf16[40,1536]{1,0:T(8,128)(2,1)} %bitcast.20, ...), custom_call_target="tpu_custom_call" | custom-call | tf_op jit(solution)/shard_map/moe/pallas_call | solution.py:397
  61.5 0.7 %copy.23 = bf16[64,1536]{1,0:T(8,128)(2,1)} copy(bf16[64,1536]{1,0:T(8,128)(2,1)S(1)} %moe.1) | data formatting | bytes 393216
